TPU v7x, 32 devices: a whole 2x2x4 slice. The times are simulated.
32 devices in a mesh: row: 8 (over z, x), mem: 2 (over core), lev: 2 (over y).
Axes of the slice: x: 2, y: 2, z: 4, core: 2. Of those that a mesh axis runs over, the one named last changes fastest.
Arguments:
- control_fields: bfloat16 [4, 6, 256, 2048], P('mem', 'lev', 'row'), may hold values from -6 to 6
- perturbations: bfloat16 [3, 4, 6, 256, 2048], P(None, 'mem', 'lev', 'row'), may hold values from -3 to 3
- column_taper: bfloat16 [2048, 2048], P('row'), may hold values from -1 to 2, as said below
- row_taper: bfloat16 [256, 256], P('row'), may hold values from -1 to 2, as said below
- courant_numbers: float32 [3, 6, 256, 2048], P(None, 'lev', 'row', 'mem'), may hold values from -0.3 to 0.3
- tracer_slope: float32 [2, 6, 256, 2048], P(None, 'lev', 'row', 'mem'), may hold values from -3 to 3
Outputs:
- increment: float32 [3, 6, 256, 2048], P(None, 'lev', 'row', 'mem')
Inputs may be any that keep to these rules, and one draw needn't show every extreme that they name: `column_taper`: A square matrix. `row_taper`: A square matrix.
All inputs are finite; a program needn't handle non-finite values.
Results may differ from a plain program's by a relative error of at most 0.0048.
Values may be sent and summed in bfloat16 or wider, within the bound.
A program may use at most 64 MiB of HBM per device.

v0:
```python
import jax
import jax.numpy as jnp
from jax import lax
from jax.experimental import pallas as pl
from jax.experimental.pallas import tpu as pltpu
from jax.sharding import PartitionSpec as P

STEPS = 4


MESH = pl.DeviceIdType.MESH
AXES = ("lev", "row", "mem")


def sides():
    found = []
    for at, axis in enumerate(AXES):
        here, count = lax.axis_index(axis), lax.axis_size(axis)
        if count > 1:
            found.append((at, 0, axis, here > 0, here - 1))
            found.append((at, 1, axis, here < count - 1, here + 1))
    return found


def advect_kernel(
    first, courant, slope, out, state, factors, level_send, row_send, level_halo, row_halo,
    column_halo, send_sem, recv_sem,
):
    kinds, levels, rows, width = first.shape
    barrier = pltpu.get_barrier_semaphore()
    neighbours = sides()
    for at, side, axis, there, target in neighbours:

        @pl.when(there)
        def _():
            pl.semaphore_signal(barrier, inc=1, device_id={axis: target}, device_id_type=MESH)

    row_at = lax.broadcasted_iota(jnp.int32, (rows, width), 0)
    column_at = lax.broadcasted_iota(jnp.int32, (rows, width), 1)
    for level in range(levels):
        centre = jnp.ones((rows, width), jnp.float32)
        for at in range(3):
            ahead = jnp.maximum(courant[at, level], 0.0)
            back = jnp.minimum(courant[at, level], 0.0)
            centre = centre - ahead + back
            if at == 1:
                ahead = jnp.where(row_at == 0, 0.0, ahead)
                back = jnp.where(row_at == rows - 1, 0.0, back)
            if at == 2:
                ahead = jnp.where(column_at == 0, 0.0, ahead)
                back = jnp.where(column_at == width - 1, 0.0, back)
            factors[1 + 2 * at, level] = ahead
            factors[2 + 2 * at, level] = back
        factors[0, level] = centre
    for kind in range(kinds):
        for level in range(levels):
            state[0, kind, level] = first[kind, level]
    pl.semaphore_wait(barrier, sum(there.astype(jnp.int32) for _, _, _, there, _ in neighbours))

    def copy_of(step, at, side, axis, target):
        if at == 0:
            source, landing = level_send.at[step, side], level_halo.at[step, 1 - side]
        elif at == 1:
            source, landing = row_send.at[step, side], row_halo.at[step, 1 - side]
        else:
            lanes = pl.ds(0 if side == 0 else width - 128, 128)
            source = state.at[step, :, :, :, lanes]
            landing = column_halo.at[step, 1 - side]
        return pltpu.make_async_remote_copy(
            src_ref=source,
            dst_ref=landing,
            send_sem=send_sem.at[step, 2 * at + side],
            recv_sem=recv_sem.at[step, 2 * at + 1 - side],
            device_id={axis: target},
            device_id_type=MESH,
        )

    def arrival(step, at, side, axis, target):
        landing = (level_halo, row_halo, column_halo)[at].at[step, side]
        return pltpu.make_async_remote_copy(
            src_ref=landing,
            dst_ref=landing,
            send_sem=send_sem.at[step, 2 * at + side],
            recv_sem=recv_sem.at[step, 2 * at + side],
            device_id={axis: target},
            device_id_type=MESH,
        )

    def one_step(step, target_ref):
        for at, side, axis, there, target in neighbours:

            @pl.when(there)
            def _():
                for kind in range(kinds):
                    if at == 0:
                        level_send[step, side, kind] = state[
                            step, kind, 0 if side == 0 else levels - 1
                        ].astype(level_send.dtype)
                    if at == 1:
                        edge = 0 if side == 0 else rows - 1
                        for level in range(levels):
                            row_send[step, side, pl.ds(kind * levels + level, 1)] = state[
                                step, kind, level, pl.ds(edge, 1)
                            ]
                copy_of(step, at, side, axis, target).start()

        for level in range(levels):
            for kind in range(kinds):
                here = state[step, kind, level]
                new = here * factors[0, level]
                new = new + factors[3, level] * pltpu.roll(here, 1, 0)
                new = new - factors[4, level] * pltpu.roll(here, rows - 1, 0)
                new = new + factors[5, level] * pltpu.roll(here, 1, 1)
                new = new - factors[6, level] * pltpu.roll(here, width - 1, 1)
                if level > 0:
                    new = new + factors[1, level] * state[step, kind, level - 1]
                if level < levels - 1:
                    new = new - factors[2, level] * state[step, kind, level + 1]
                if kind == 2:
                    new = new - (
                        state[step, 0, level] * slope[0, level]
                        + state[step, 1, level] * slope[1, level]
                    )
                target_ref[kind, level] = new

        lane_at = lax.broadcasted_iota(jnp.int32, (rows, 128), 1)
        for at, side, axis, there, target in (
            [n for n in neighbours if n[0] == 2]
            + [n for n in neighbours if n[0] == 1]
            + [n for n in neighbours if n[0] == 0]
        ):

            @pl.when(there)
            def _():
                arrival(step, at, side, axis, target).wait_recv()
                for kind in range(kinds):
                    if at == 0:
                        level = 0 if side == 0 else levels - 1
                        term = factors[1 + side, level] * level_halo[step, side, kind].astype(
                            jnp.float32
                        )
                        if side:
                            term = -term
                        target_ref[kind, level] = target_ref[kind, level] + term
                        continue
                    for level in range(levels):
                        if at == 1:
                            edge = pl.ds(0 if side == 0 else rows - 1, 1)
                            speed = courant[1, level, edge]
                            speed = jnp.minimum(speed, 0.0) if side else jnp.maximum(speed, 0.0)
                            term = speed * row_halo[step, side, pl.ds(kind * levels + level, 1)]
                            if side:
                                term = -term
                            target_ref[kind, level, edge] = target_ref[kind, level, edge] + term
                        else:
                            lanes = pl.ds(width - 128 if side else 0, 128)
                            speed = courant[2, level, :, lanes]
                            speed = jnp.minimum(speed, 0.0) if side else jnp.maximum(speed, 0.0)
                            beside = pltpu.roll(
                                column_halo[step, side, kind, level], 127 if side else 1, 1
                            )
                            term = jnp.where(
                                lane_at == (127 if side else 0), speed * beside, 0.0
                            )
                            if side:
                                term = -term
                            target_ref[kind, level, :, lanes] = (
                                target_ref[kind, level, :, lanes] + term
                            )

    @pl.loop(0, STEPS - 1)
    def _(step):
        one_step(step, state.at[step + 1])

    one_step(STEPS - 1, out)

    @pl.loop(0, STEPS)
    def _(step):
        for at, side, axis, there, target in neighbours:

            @pl.when(there)
            def _():
                copy_of(step, at, side, axis, target).wait_send()


def advected(weighted, courant_numbers, tracer_slope):
    kinds, levels, rows, width = weighted.shape
    edges = -(-kinds * levels // 8) * 8
    return pl.pallas_call(
        advect_kernel,
        out_shape=jax.ShapeDtypeStruct(weighted.shape, jnp.float32),
        in_specs=[pl.BlockSpec(memory_space=pltpu.VMEM)] * 3,
        out_specs=pl.BlockSpec(memory_space=pltpu.VMEM),
        scratch_shapes=[
            pltpu.VMEM((STEPS, kinds, levels, rows, width), jnp.float32),
            pltpu.VMEM((7, levels, rows, width), jnp.float32),
            pltpu.VMEM((STEPS, 2, kinds, rows, width), jnp.bfloat16),
            pltpu.VMEM((STEPS, 2, edges, width), jnp.float32),
            pltpu.VMEM((STEPS, 2, kinds, rows, width), jnp.bfloat16),
            pltpu.VMEM((STEPS, 2, edges, width), jnp.float32),
            pltpu.VMEM((STEPS, 2, kinds, levels, rows, 128), jnp.float32),
            pltpu.SemaphoreType.DMA((STEPS, 6)),
            pltpu.SemaphoreType.DMA((STEPS, 6)),
        ],
        compiler_params=pltpu.CompilerParams(
            collective_id=1, has_side_effects=True, vmem_limit_bytes=48 << 20
        ),
        name="advect",
    )(weighted, courant_numbers, tracer_slope)


def localize_kernel(
    control, pert, taper, row_part, out, gathered, row_all, staged, halves, taper_all, pert_all,
    total, one_send, one_recv, row_send, row_recv, two_send, two_recv, pass_send, pass_recv,
    pert_send, pert_recv, ring_send, ring_recv, lev_send, lev_recv, own_sem,
):
    count, mems, levs = (lax.axis_size(axis) for axis in ("row", "mem", "lev"))
    me, mem_at, lev_at = (lax.axis_index(axis) for axis in ("row", "mem", "lev"))
    fields, rows, depth = control.shape[1:]
    kinds, members, levels = pert.shape[:3]
    width = out.shape[3]
    chains = ring_send.shape[0]
    lanes, share = width // chains, depth // levs
    half = count // 2

    def order(place):
        place = (place + 2 * count) % count
        late = place // half
        return (1 - late) * 2 * place + late * (2 * (count - 1 - place) + 1)

    place = (1 - me % 2) * (me // 2) + (me % 2) * (count - 1 - me // 2)

    def remote(source, landing, sent, landed, **target):
        return pltpu.make_async_remote_copy(
            src_ref=source, dst_ref=landing, send_sem=sent, recv_sem=landed,
            device_id=target, device_id_type=MESH,
        )

    def own_columns(at):
        return pl.ds(pl.multiple_of(at * width, width), width)

    def one(peer, slot):
        return remote(control.at[peer], gathered.at[slot], one_send.at[peer], one_recv.at[slot], row=peer)

    def row(peer, slot):
        return remote(row_part, row_all.at[slot], row_send.at[peer], row_recv.at[slot], row=peer)

    def two(peer, slot):
        return remote(
            staged.at[peer], halves.at[mem_at, slot], two_send.at[peer], two_recv.at[slot], row=peer
        )

    def onward(peer, slot, place_of):
        return remote(
            halves.at[place_of, slot], halves.at[place_of, slot], pass_send.at[peer, slot],
            pass_recv.at[place_of, slot], mem=peer,
        )

    def pert_copy(peer, slot):
        return remote(
            pert.at[:, :, :, :, own_columns(peer)], pert_all.at[slot], pert_send.at[peer],
            pert_recv.at[slot], mem=peer,
        )

    def piece(chain, origin, lev):
        return taper_all.at[
            origin, pl.ds(pl.multiple_of(lev * share, share), share), pl.ds(chain * lanes, lanes)
        ]

    def ring(chain, hop, sending):
        way = 1 - 2 * (chain % 2)
        origin = order(place - way * hop) if sending else order(place - way * (hop + 1))
        part = piece(chain, origin, lev_at)
        return remote(part, part, ring_send.at[chain, hop], ring_recv.at[chain, hop], row=order(place + way))

    def across(chain, hop, shift, sending):
        way = 1 - 2 * (chain % 2)
        origin = order(place - way * (hop + 1))
        peer = (lev_at + shift) % levs
        source = (lev_at + levs - shift) % levs
        part = piece(chain, origin, lev_at if sending else source)
        return remote(
            part, part, lev_send.at[chain, hop, shift - 1], lev_recv.at[chain, hop, shift - 1], lev=peer
        )

    def ring_step(hop, last):
        for chain in range(chains):
            ring(chain, hop - 1, False).wait_recv()
            if not last:
                ring(chain, hop, True).start()
            for shift in range(1, levs):
                across(chain, hop - 1, shift, True).start()

    barrier = pltpu.get_barrier_semaphore()
    for axis, here, size in (("row", me, count), ("mem", mem_at, mems), ("lev", lev_at, levs)):

        @pl.loop(1, size)
        def _(shift):
            pl.semaphore_signal(
                barrier, inc=1, device_id={axis: (here + shift) % size}, device_id_type=MESH
            )

    own_taper = pltpu.make_async_copy(taper.at[:, own_columns(mem_at)], taper_all.at[me], own_sem.at[0])
    own_taper.start()
    own_pert = pltpu.make_async_copy(
        pert.at[:, :, :, :, own_columns(mem_at)], pert_all.at[mem_at], own_sem.at[1]
    )
    own_pert.start()
    gathered[me] = control[me]
    row_all[me] = row_part[...]
    own_taper.wait()
    pl.semaphore_wait(barrier, count + mems + levs - 3)

    for chain in range(chains):
        ring(chain, 0, True).start()

    @pl.loop(1, count)
    def _(shift):
        peer = (me + shift) % count
        row(peer, me).start()
        one(peer, me).start()

    @pl.loop(1, mems)
    def _(shift):
        pert_copy((mem_at + shift) % mems, mem_at).start()

    early = max(1, min(3, count - 2))
    for hop in range(1, early + 1):
        ring_step(hop, count == 2)

    @pl.loop(1, count)
    def _(shift):
        peer = (me + shift) % count
        row(peer, peer).wait_recv()
        one(peer, peer).wait_recv()

    row_whole = row_all[...].reshape(count * rows, count * rows)

    @pl.loop(0, fields)
    def _(field):
        tapered = jnp.dot(
            row_whole,
            gathered[:, field].reshape(count * rows, depth),
            preferred_element_type=jnp.float32,
        )
        staged[:, field] = tapered.astype(jnp.bfloat16).reshape(count, rows, depth)

    @pl.loop(1, count)
    def _(shift):
        two((me + shift) % count, me).start()

    halves[mem_at, me] = staged[me]

    @pl.loop(1, mems)
    def _(shift):
        onward((mem_at + shift) % mems, me, mem_at).start()

    if count > 2:

        @pl.loop(early + 1, count - 1)
        def _(hop):
            ring_step(hop, False)

        ring_step(count - 1, True)

    @pl.loop(1, count)
    def _(shift):
        slot = (me + shift) % count
        two(slot, slot).wait_recv()

        @pl.loop(1, mems)
        def _(step):
            onward((mem_at + step) % mems, slot, mem_at).start()

    @pl.loop(1, mems)
    def _(step):
        peer = (mem_at + step) % mems
        pert_copy(peer, peer).wait_recv()

        @pl.loop(0, count)
        def _(slot):
            onward(peer, slot, peer).wait_recv()

    @pl.loop(0, count - 1)
    def _(hop):
        for chain in range(chains):
            for shift in range(1, levs):
                across(chain, hop, shift, False).wait_recv()

    total[...] = jnp.zeros_like(total)

    @pl.loop(0, count)
    def _(slot):
        total[...] += jnp.dot(
            halves[:, slot].reshape(mems * fields * rows, depth),
            taper_all[slot],
            preferred_element_type=jnp.float32,
        )

    own_pert.wait()
    for level in range(levels):
        for kind in range(kinds):
            weighted = jnp.zeros((rows, width), jnp.float32)
            for mem in range(mems):
                for member in range(members):
                    at = ((mem * members + member) * levels + level) * rows
                    weighted = weighted + pert_all[mem, kind, member, level].astype(
                        jnp.float32
                    ) * total[pl.ds(at, rows)]
            out[kind, level] = weighted

    @pl.loop(1, count)
    def _(shift):
        peer = (me + shift) % count
        row(peer, me).wait_send()
        one(peer, me).wait_send()
        two(peer, me).wait_send()

    @pl.loop(1, mems)
    def _(shift):
        peer = (mem_at + shift) % mems
        pert_copy(peer, mem_at).wait_send()

        @pl.loop(0, count)
        def _(slot):
            onward(peer, slot, mem_at).wait_send()

    @pl.loop(0, count - 1)
    def _(hop):
        for chain in range(chains):
            ring(chain, hop, True).wait_send()
            for shift in range(1, levs):
                across(chain, hop, shift, True).wait_send()


def localized(control_fields, perturbations, column_taper, row_taper):
    members, levels, rows, columns = control_fields.shape
    kinds = perturbations.shape[0]
    count, mems, levs = (lax.axis_size(axis) for axis in ("row", "mem", "lev"))
    fields, depth, width = members * levels, columns // count, columns // mems
    split = control_fields.reshape(fields, rows, count, depth).transpose(2, 0, 1, 3)
    chains = 4 if width % 512 == 0 else 2
    low, dma = jnp.bfloat16, pltpu.SemaphoreType.DMA
    return pl.pallas_call(
        localize_kernel,
        out_shape=jax.ShapeDtypeStruct((kinds, levels, rows, width), jnp.float32),
        in_specs=[pl.BlockSpec(memory_space=pltpu.VMEM)] * 4,
        out_specs=pl.BlockSpec(memory_space=pltpu.VMEM),
        scratch_shapes=[
            pltpu.VMEM((count, fields, rows, depth), low),
            pltpu.VMEM((count, rows, count * rows), low),
            pltpu.VMEM((count, fields, rows, depth), low),
            pltpu.VMEM((mems, count, fields, rows, depth), low),
            pltpu.VMEM((count, depth, width), low),
            pltpu.VMEM((mems, kinds, members, levels, rows, width), low),
            pltpu.VMEM((mems * fields * rows, width), jnp.float32),
            dma((count,)), dma((count,)), dma((count,)), dma((count,)), dma((count,)), dma((count,)),
            dma((mems, count)), dma((mems, count)), dma((mems,)), dma((mems,)),
            dma((chains, count)), dma((chains, count)),
            dma((chains, count, levs)), dma((chains, count, levs)), dma((2,)),
        ],
        compiler_params=pltpu.CompilerParams(
            collective_id=0, has_side_effects=True, vmem_limit_bytes=56 << 20
        ),
        name="localize",
    )(split, perturbations, column_taper, row_taper)


def on_device(
    control_fields, perturbations, column_taper, row_taper, courant_numbers, tracer_slope
):
    weighted = localized(control_fields, perturbations, column_taper, row_taper)
    return advected(weighted, courant_numbers, tracer_slope)


def solution(mesh):
    placed = (
        P("mem", "lev", "row", None),
        P(None, "mem", "lev", "row", None),
        P("row", None),
        P("row", None),
        P(None, "lev", "row", "mem"),
        P(None, "lev", "row", "mem"),
    )
    return jax.shard_map(
        on_device,
        mesh=mesh,
        in_specs=placed,
        out_specs=P(None, "lev", "row", "mem"),
        check_vma=False,
    )
```

profile of v0, /device:TPU:0, one launch (start us, length us, event | category | flops | bytes accessed | tf_op | source)
XLA Modules:
  0.0 109.9 jit_solution(2928373905273837064)
XLA Ops:
  0.0 1.3 %copy.8 = bf16[24,8,8,256]{3,2,1,0:T(8,128)(2,1)S(1)} copy(bf16[24,8,8,256]{3,1,2,0:T(8,128)(2,1)} %bitcast.10) | data formatting | bytes 1572864
  1.3 1.1 copy.10
  2.4 0.0 copy-start.1
  2.4 0.0 copy-start.2
  2.4 80.2 %localize.1.first = f32[3,3,32,1024]{3,2,1,0:T(8,128)} custom-call(bf16[8,6,32,256]{3,2,1,0:T(8,128)(2,1)} %bitcast.9, bf16[3,2,3,32,2048]{4,3,2,1,0:T(8,128)(2,1)} %pert.1, bf16[256,2048]{1,0:T(8,128)(2,1)} %taper.1, bf16[32,256]{1,0:T(8,128)(2,1)} %row_part.1), custom_call_target="tpu_custom_call" | custom-call | tf_op jit(solution)/shard_map/localize/pallas_call | solution.py:444
  82.6 0.0 copy-done.1
  82.6 0.0 copy-done.2
  82.6 0.0 copy-start
  82.6 1.3 %copy-done = f32[3,3,32,1024]{3,2,1,0:T(8,128)S(1)} copy-done((f32[3,3,32,1024]{3,2,1,0:T(8,128)S(1)}, f32[3,3,32,1024]{3,2,1,0:T(8,128)}, u32[]{:S(2)}) %copy-start) | copy-done | bytes 1179672
  83.9 24.9 %advect.1 = f32[3,3,32,1024]{3,2,1,0:T(8,128)S(1)} custom-call(f32[3,3,32,1024]{3,2,1,0:T(8,128)S(1)} %copy-done, f32[3,3,32,1024]{3,2,1,0:T(8,128)S(1)} %copy-done.1, f32[2,3,32,1024]{3,2,1,0:T(8,128)S(1)} %copy-done.2), custom_call_target="tpu_custom_call" | custom-call | tf_op jit(solution)/shard_map/advect/pallas_call | solution.py:189
  108.9 1.0 copy.12
Async XLA Ops:
  2.4 80.2 %copy-start.1 = (f32[3,3,32,1024]{3,2,1,0:T(8,128)S(1)}, f32[3,3,32,1024]{3,2,1,0:T(8,128)}, u32[]{:S(2)}) copy-start(f32[3,3,32,1024]{3,2,1,0:T(8,128)} %courant.1) | copy-start | bytes 3538948
  2.4 80.2 %copy-start.2 = (f32[2,3,32,1024]{3,2,1,0:T(8,128)S(1)}, f32[2,3,32,1024]{3,2,1,0:T(8,128)}, u32[]{:S(2)}) copy-start(f32[2,3,32,1024]{3,2,1,0:T(8,128)} %slope.1) | copy-start | bytes 2359300
  82.6 1.3 %copy-start = (f32[3,3,32,1024]{3,2,1,0:T(8,128)S(1)}, f32[3,3,32,1024]{3,2,1,0:T(8,128)}, u32[]{:S(2)}) copy-start(f32[3,3,32,1024]{3,2,1,0:T(8,128)} %localize.1.first) | copy-start | bytes 3538948
where the time goes:
time: 110 us
  Pallas kernels  105 us (95%)
  local copies, waits for them, and re-layouts  4.67 us (4%)
    pallas_call x1, Pallas kernels, localized(): pl.pallas_call(localize_kernel, out_shape=jax.ShapeDtypeStruct((kinds, le...  80.2 us
    pallas_call x1, Pallas kernels, advected(): pl.pallas_call(advect_kernel, out_shape=jax.ShapeDtypeStruct(weighted.sha...  24.9 us
    unnamed x8, local copies, waits for them, and re-layouts  3.61 us

commit v1 on v0

--- a/solution.py
+++ b/solution.py
@@ -210,50 +210,72 @@
 
 
 def localize_kernel(
-    control, pert, taper, row_part, out, gathered, row_all, staged, halves, taper_all, pert_all,
-    total, one_send, one_recv, row_send, row_recv, two_send, two_recv, pass_send, pass_recv,
-    pert_send, pert_recv, ring_send, ring_recv, lev_send, lev_recv, own_sem,
+    control, pert, taper, row_part, out, own, gathered, row_all, staged, halves, taper_all, pert_all,
+    one_send, one_recv, row_send, row_recv, two_send, two_recv, pass_send, pass_recv, pert_send,
+    pert_recv, first_send, first_recv, line_send, line_recv, side_send, side_recv, lev_send, lev_recv,
+    own_sem,
 ):
     count, mems, levs = (lax.axis_size(axis) for axis in ("row", "mem", "lev"))
     me, mem_at, lev_at = (lax.axis_index(axis) for axis in ("row", "mem", "lev"))
-    fields, rows, depth = control.shape[1:]
-    kinds, members, levels = pert.shape[:3]
-    width = out.shape[3]
-    chains = ring_send.shape[0]
-    lanes, share = width // chains, depth // levs
-    half = count // 2
-
-    def order(place):
-        place = (place + 2 * count) % count
-        late = place // half
-        return (1 - late) * 2 * place + late * (2 * (count - 1 - place) + 1)
-
-    place = (1 - me % 2) * (me // 2) + (me % 2) * (count - 1 - me // 2)
-
-    def remote(source, landing, sent, landed, **target):
+    kinds, members, levels, rows, columns = pert.shape
+    depth, width = taper.shape[0], out.shape[3]
+    inner = 2 if count % 2 == 0 else 1
+    outer = count // inner
+    line_at, side_at = me // inner, me % inner
+    share, lanes = depth // levs, width // inner
+    sent = []
+
+    def remote(source, landing, to, at, **target):
         return pltpu.make_async_remote_copy(
-            src_ref=source, dst_ref=landing, send_sem=sent, recv_sem=landed,
-            device_id=target, device_id_type=MESH,
-        )
+            src_ref=source, dst_ref=landing, send_sem=to, recv_sem=at, device_id=target,
+            device_id_type=MESH,
+        )
+
+    def send(there, copy):
+        sent.append((there, copy))
+        when(there, lambda: copy().start())
+
+    def when(there, action):
+        if there is True:
+            action()
+        else:
+            pl.when(there)(action)
 
     def own_columns(at):
         return pl.ds(pl.multiple_of(at * width, width), width)
 
-    def one(peer, slot):
-        return remote(control.at[peer], gathered.at[slot], one_send.at[peer], one_recv.at[slot], row=peer)
+    def block(source, at, level):
+        if len(source.shape) == 5:
+            return source.at[at, :, level]
+        return source.at[:, level, :, pl.ds(pl.multiple_of(at * depth, depth), depth)]
+
+    def level_of(turn):
+        return jnp.where(lev_at > 0, turn, levels - 1 - turn)
+
+    offsets = sorted(range(1, count), key=lambda by: -min(by // inner, outer - by // inner))
+
+    def peer_of(by):
+        return (line_at + by // inner) % outer * inner + (side_at + by % inner) % inner
+
+    def one(peer, slot, level):
+        return remote(
+            block(own, peer, level), gathered.at[slot, level], one_send.at[peer, level],
+            one_recv.at[slot, level], row=peer,
+        )
 
     def row(peer, slot):
-        return remote(row_part, row_all.at[slot], row_send.at[peer], row_recv.at[slot], row=peer)
-
-    def two(peer, slot):
+        return remote(row_all.at[me], row_all.at[slot], row_send.at[peer], row_recv.at[slot], row=peer)
+
+    def two(peer, slot, level):
         return remote(
-            staged.at[peer], halves.at[mem_at, slot], two_send.at[peer], two_recv.at[slot], row=peer
-        )
-
-    def onward(peer, slot, place_of):
+            staged.at[peer, level], halves.at[level, slot, mem_at], two_send.at[peer, level],
+            two_recv.at[slot, level], row=peer,
+        )
+
+    def onward(peer, slot, level, place):
+        part = halves.at[level, slot, place]
         return remote(
-            halves.at[place_of, slot], halves.at[place_of, slot], pass_send.at[peer, slot],
-            pass_recv.at[place_of, slot], mem=peer,
+            part, part, pass_send.at[peer, slot, level], pass_recv.at[place, slot, level], mem=peer
         )
 
     def pert_copy(peer, slot):
@@ -262,34 +284,82 @@
             pert_recv.at[slot], mem=peer,
         )
 
-    def piece(chain, origin, lev):
+    def piece(origin, lev, side):
         return taper_all.at[
-            origin, pl.ds(pl.multiple_of(lev * share, share), share), pl.ds(chain * lanes, lanes)
+            origin,
+            pl.ds(pl.multiple_of(lev * share, share), share),
+            pl.ds(pl.multiple_of(side * lanes, lanes), lanes),
         ]
 
-    def ring(chain, hop, sending):
-        way = 1 - 2 * (chain % 2)
-        origin = order(place - way * hop) if sending else order(place - way * (hop + 1))
-        part = piece(chain, origin, lev_at)
-        return remote(part, part, ring_send.at[chain, hop], ring_recv.at[chain, hop], row=order(place + way))
-
-    def across(chain, hop, shift, sending):
-        way = 1 - 2 * (chain % 2)
-        origin = order(place - way * (hop + 1))
-        peer = (lev_at + shift) % levs
-        source = (lev_at + levs - shift) % levs
-        part = piece(chain, origin, lev_at if sending else source)
+    other = line_at * inner + (inner - 1 - side_at)
+
+    def first(origin, side):
+        part = piece(origin, lev_at, side)
+        return remote(part, part, first_send.at[0], first_recv.at[0], row=other)
+
+    def side(origin, at):
+        part = piece(origin, lev_at, at)
+        return remote(part, part, side_send.at[origin], side_recv.at[origin], row=other)
+
+    def line(way, hop, turn, sending):
+        back = hop if sending else hop + 1
+        from_line = line_at - back if way == 0 else line_at + back
+        to_line = line_at + 1 if way == 0 else line_at - 1
+        origin = from_line * inner + (side_at if turn == 0 else inner - 1 - side_at)
+        there = from_line >= 0 if way == 0 else from_line <= outer - 1
+        if sending:
+            there = there & (to_line <= outer - 1 if way == 0 else to_line >= 0)
+
+        def copy():
+            part = piece(origin, lev_at, side_at)
+            return remote(
+                part, part, line_send.at[way, hop, turn], line_recv.at[way, hop, turn],
+                row=to_line * inner + side_at,
+            )
+
+        return origin, there, copy
+
+    def lev_copy(origin, at, shift, sending):
+        part = piece(origin, lev_at if sending else (lev_at + levs - shift) % levs, at)
         return remote(
-            part, part, lev_send.at[chain, hop, shift - 1], lev_recv.at[chain, hop, shift - 1], lev=peer
-        )
-
-    def ring_step(hop, last):
-        for chain in range(chains):
-            ring(chain, hop - 1, False).wait_recv()
-            if not last:
-                ring(chain, hop, True).start()
-            for shift in range(1, levs):
-                across(chain, hop - 1, shift, True).start()
+            part, part, lev_send.at[origin, at, shift - 1], lev_recv.at[origin, at, shift - 1],
+            lev=(lev_at + shift) % levs,
+        )
+
+    def across(there, origin, at):
+        for shift in range(1, levs):
+            send(there, lambda shift=shift: lev_copy(origin, at, shift, True))
+
+    def along_line(hop, turn):
+        if outer == 1:
+            return
+        for way in range(2):
+            _, there, copy = line(way, hop, turn, True)
+            send(there, copy)
+
+    def one_chunk(turn):
+        level = level_of(turn)
+        for by in offsets:
+            send(True, lambda by=by: one(peer_of(by), me, level))
+
+    def row_step(turn):
+        level = level_of(turn)
+        for by in offsets:
+            slot = peer_of(by)
+            one(slot, slot, level).wait_recv()
+        whole = row_all[...].reshape(count * rows, count * rows)
+        for member in range(members):
+            tapered = jnp.dot(
+                whole, gathered[:, level, member].reshape(count * rows, depth),
+                preferred_element_type=jnp.float32,
+            )
+            staged[:, level, member] = tapered.astype(jnp.bfloat16).reshape(count, rows, depth)
+        for by in offsets:
+            send(True, lambda by=by: two(peer_of(by), me, level))
+        for member in range(members):
+            halves[level, me, mem_at, member] = staged[me, level, member]
+        for shift in range(1, mems):
+            send(True, lambda shift=shift: onward((mem_at + shift) % mems, me, level, mem_at))
 
     barrier = pltpu.get_barrier_semaphore()
     for axis, here, size in (("row", me, count), ("mem", mem_at, mems), ("lev", lev_at, levs)):
@@ -300,170 +370,178 @@
                 barrier, inc=1, device_id={axis: (here + shift) % size}, device_id_type=MESH
             )
 
-    own_taper = pltpu.make_async_copy(taper.at[:, own_columns(mem_at)], taper_all.at[me], own_sem.at[0])
-    own_taper.start()
-    own_pert = pltpu.make_async_copy(
-        pert.at[:, :, :, :, own_columns(mem_at)], pert_all.at[mem_at], own_sem.at[1]
-    )
-    own_pert.start()
-    gathered[me] = control[me]
-    row_all[me] = row_part[...]
-    own_taper.wait()
+    fetches = [
+        pltpu.make_async_copy(taper.at[:, own_columns(mem_at)], taper_all.at[me], own_sem.at[0]),
+        pltpu.make_async_copy(control, own, own_sem.at[1]),
+        pltpu.make_async_copy(row_part, row_all.at[me], own_sem.at[2]),
+        pltpu.make_async_copy(
+            pert.at[:, :, :, :, own_columns(mem_at)], pert_all.at[mem_at], own_sem.at[3]
+        ),
+    ]
+    for level in range(levels):
+        fetches.append(
+            pltpu.make_async_copy(
+                block(control, me, level), gathered.at[me, level], own_sem.at[4 + level]
+            )
+        )
+    for fetch in fetches:
+        fetch.start()
+    for fetch in fetches[:3]:
+        fetch.wait()
     pl.semaphore_wait(barrier, count + mems + levs - 3)
 
-    for chain in range(chains):
-        ring(chain, 0, True).start()
-
-    @pl.loop(1, count)
-    def _(shift):
-        peer = (me + shift) % count
-        row(peer, me).start()
-        one(peer, me).start()
-
-    @pl.loop(1, mems)
-    def _(shift):
-        pert_copy((mem_at + shift) % mems, mem_at).start()
-
-    early = max(1, min(3, count - 2))
-    for hop in range(1, early + 1):
-        ring_step(hop, count == 2)
-
-    @pl.loop(1, count)
-    def _(shift):
-        peer = (me + shift) % count
-        row(peer, peer).wait_recv()
-        one(peer, peer).wait_recv()
-
-    row_whole = row_all[...].reshape(count * rows, count * rows)
-
-    @pl.loop(0, fields)
-    def _(field):
-        tapered = jnp.dot(
-            row_whole,
-            gathered[:, field].reshape(count * rows, depth),
-            preferred_element_type=jnp.float32,
-        )
-        staged[:, field] = tapered.astype(jnp.bfloat16).reshape(count, rows, depth)
-
-    @pl.loop(1, count)
-    def _(shift):
-        two((me + shift) % count, me).start()
-
-    halves[mem_at, me] = staged[me]
-
-    @pl.loop(1, mems)
-    def _(shift):
-        onward((mem_at + shift) % mems, me, mem_at).start()
-
-    if count > 2:
-
-        @pl.loop(early + 1, count - 1)
-        def _(hop):
-            ring_step(hop, False)
-
-        ring_step(count - 1, True)
-
-    @pl.loop(1, count)
-    def _(shift):
-        slot = (me + shift) % count
-        two(slot, slot).wait_recv()
-
-        @pl.loop(1, mems)
-        def _(step):
-            onward((mem_at + step) % mems, slot, mem_at).start()
-
-    @pl.loop(1, mems)
-    def _(step):
-        peer = (mem_at + step) % mems
+    if inner > 1:
+        send(True, lambda: first(me, inner - 1 - side_at))
+    along_line(0, 0)
+    if inner > 1:
+        send(True, lambda: side(me, side_at))
+    for by in offsets:
+        send(True, lambda by=by: row(peer_of(by), me))
+    one_chunk(0)
+    for shift in range(1, mems):
+        send(True, lambda shift=shift: pert_copy((mem_at + shift) % mems, mem_at))
+    for fetch in fetches[3:]:
+        fetch.wait()
+    if inner > 1:
+        first(other, side_at).wait_recv()
+        along_line(0, 1)
+        across(True, other, side_at)
+    for turn in range(1, levels - 1):
+        one_chunk(turn)
+    if inner > 1:
+        side(other, inner - 1 - side_at).wait_recv()
+        across(True, other, inner - 1 - side_at)
+
+    def hop_step(hop):
+        for turn in range(inner):
+            for way in range(2):
+                origin, there, copy = line(way, hop, turn, False)
+
+                def arrived(copy=copy):
+                    copy().wait_recv()
+
+                when(there, arrived)
+                if hop + 1 < outer - 1:
+                    _, onwards, relay = line(way, hop + 1, turn, True)
+                    send(onwards, relay)
+                if inner > 1:
+                    send(there, lambda origin=origin: side(origin, side_at))
+                across(there, origin, side_at)
+
+    def side_step(hop):
+        for turn in range(inner):
+            for way in range(2):
+                origin, there, _ = line(way, hop, turn, False)
+                if inner > 1:
+
+                    def arrived(origin=origin):
+                        side(origin, inner - 1 - side_at).wait_recv()
+
+                    when(there, arrived)
+                    across(there, origin, inner - 1 - side_at)
+
+    ready = 0
+    for hop in range(outer - 1):
+        hop_step(hop)
+        if hop == 0:
+            one_chunk(levels - 1)
+            for by in offsets:
+                slot = peer_of(by)
+                row(slot, slot).wait_recv()
+        if ready < levels:
+            row_step(ready)
+            ready += 1
+        side_step(hop)
+    for turn in range(ready, levels):
+        row_step(turn)
+
+    for turn in range(levels):
+        level = level_of(turn)
+        for by in offsets:
+            slot = peer_of(by)
+            two(slot, slot, level).wait_recv()
+            for shift in range(1, mems):
+                send(
+                    True,
+                    lambda shift=shift, slot=slot, level=level: onward(
+                        (mem_at + shift) % mems, slot, level, mem_at
+                    ),
+                )
+
+    for by in offsets:
+        origin = peer_of(by)
+        for at in range(inner):
+            for shift in range(1, levs):
+                lev_copy(origin, at, shift, False).wait_recv()
+    for shift in range(1, mems):
+        peer = (mem_at + shift) % mems
         pert_copy(peer, peer).wait_recv()
 
-        @pl.loop(0, count)
-        def _(slot):
-            onward(peer, slot, peer).wait_recv()
-
-    @pl.loop(0, count - 1)
-    def _(hop):
-        for chain in range(chains):
-            for shift in range(1, levs):
-                across(chain, hop, shift, False).wait_recv()
-
-    total[...] = jnp.zeros_like(total)
-
-    @pl.loop(0, count)
-    def _(slot):
-        total[...] += jnp.dot(
-            halves[:, slot].reshape(mems * fields * rows, depth),
-            taper_all[slot],
-            preferred_element_type=jnp.float32,
-        )
-
-    own_pert.wait()
-    for level in range(levels):
-        for kind in range(kinds):
-            weighted = jnp.zeros((rows, width), jnp.float32)
-            for mem in range(mems):
-                for member in range(members):
-                    at = ((mem * members + member) * levels + level) * rows
-                    weighted = weighted + pert_all[mem, kind, member, level].astype(
-                        jnp.float32
-                    ) * total[pl.ds(at, rows)]
-            out[kind, level] = weighted
-
-    @pl.loop(1, count)
-    def _(shift):
-        peer = (me + shift) % count
-        row(peer, me).wait_send()
-        one(peer, me).wait_send()
-        two(peer, me).wait_send()
-
-    @pl.loop(1, mems)
-    def _(shift):
-        peer = (mem_at + shift) % mems
-        pert_copy(peer, mem_at).wait_send()
-
-        @pl.loop(0, count)
-        def _(slot):
-            onward(peer, slot, mem_at).wait_send()
-
-    @pl.loop(0, count - 1)
-    def _(hop):
-        for chain in range(chains):
-            ring(chain, hop, True).wait_send()
-            for shift in range(1, levs):
-                across(chain, hop, shift, True).wait_send()
+    span = min(width, 256)
+    for turn in range(levels):
+        level = level_of(turn)
+        for shift in range(1, mems):
+            peer = (mem_at + shift) % mems
+
+            @pl.loop(0, count)
+            def _(slot):
+                onward(peer, slot, level, peer).wait_recv()
+
+        for start in range(0, width, span):
+            total = jnp.zeros((mems * members * rows, span), jnp.float32)
+            for slot in range(count):
+                total = total + jnp.dot(
+                    halves[level, slot].reshape(mems * members * rows, depth),
+                    taper_all[slot, :, pl.ds(start, span)],
+                    preferred_element_type=jnp.float32,
+                )
+            for kind in range(kinds):
+                weighted = jnp.zeros((rows, span), jnp.float32)
+                for mem in range(mems):
+                    for member in range(members):
+                        at = (mem * members + member) * rows
+                        weighted = weighted + pert_all[
+                            mem, kind, member, level, :, pl.ds(start, span)
+                        ].astype(jnp.float32) * total[at : at + rows]
+                out[kind, level, :, pl.ds(start, span)] = weighted
+
+    for there, copy in sent:
+        when(there, lambda copy=copy: copy().wait_send())
 
 
 def localized(control_fields, perturbations, column_taper, row_taper):
     members, levels, rows, columns = control_fields.shape
     kinds = perturbations.shape[0]
     count, mems, levs = (lax.axis_size(axis) for axis in ("row", "mem", "lev"))
-    fields, depth, width = members * levels, columns // count, columns // mems
-    split = control_fields.reshape(fields, rows, count, depth).transpose(2, 0, 1, 3)
-    chains = 4 if width % 512 == 0 else 2
+    depth, width = columns // count, columns // mems
+    if depth % 128:
+        control_fields = control_fields.reshape(members, levels, rows, count, depth)
+        control_fields = control_fields.transpose(3, 0, 1, 2, 4)
     low, dma = jnp.bfloat16, pltpu.SemaphoreType.DMA
+    pairs = [dma((count, levels))] * 2 + [dma((count,))] * 2 + [dma((count, levels))] * 2
+    pairs += [dma((mems, count, levels))] * 2 + [dma((mems,))] * 2 + [dma((1,))] * 2
+    pairs += [dma((2, count, 2))] * 2 + [dma((count,))] * 2 + [dma((count, 2, levs))] * 2
     return pl.pallas_call(
         localize_kernel,
         out_shape=jax.ShapeDtypeStruct((kinds, levels, rows, width), jnp.float32),
-        in_specs=[pl.BlockSpec(memory_space=pltpu.VMEM)] * 4,
+        in_specs=[pl.BlockSpec(memory_space=pl.ANY)] * 4,
         out_specs=pl.BlockSpec(memory_space=pltpu.VMEM),
         scratch_shapes=[
-            pltpu.VMEM((count, fields, rows, depth), low),
+            pltpu.VMEM(control_fields.shape, low),
+            pltpu.VMEM((count, levels, members, rows, depth), low),
             pltpu.VMEM((count, rows, count * rows), low),
-            pltpu.VMEM((count, fields, rows, depth), low),
-            pltpu.VMEM((mems, count, fields, rows, depth), low),
+            pltpu.VMEM((count, levels, members, rows, depth), low),
+            pltpu.VMEM((levels, count, mems, members, rows, depth), low),
             pltpu.VMEM((count, depth, width), low),
             pltpu.VMEM((mems, kinds, members, levels, rows, width), low),
-            pltpu.VMEM((mems * fields * rows, width), jnp.float32),
-            dma((count,)), dma((count,)), dma((count,)), dma((count,)), dma((count,)), dma((count,)),
-            dma((mems, count)), dma((mems, count)), dma((mems,)), dma((mems,)),
-            dma((chains, count)), dma((chains, count)),
-            dma((chains, count, levs)), dma((chains, count, levs)), dma((2,)),
+            *pairs,
+            dma((4 + levels,)),
         ],
         compiler_params=pltpu.CompilerParams(
             collective_id=0, has_side_effects=True, vmem_limit_bytes=56 << 20
         ),
         name="localize",
-    )(split, perturbations, column_taper, row_taper)
+    )(control_fields, perturbations, column_taper, row_taper)
 
 
 def on_device(

time: 110 us -> 95.1 us (0.86)
  Pallas kernels: 105 us -> 92.6 us
  local copies, waits for them, and re-layouts: 4.67 us -> 2.29 us
    pallas_call x1, Pallas kernels: 80.2 us -> 68.9 us  [localized(): pl.pallas_call(localize_kernel, out_shape=jax.ShapeDtypeStruct((kinds, le...]
    unnamed x8 -> x7, local copies, waits for them, and re-layouts: 3.61 us -> 2.29 us
    pallas_call x1, Pallas kernels: 24.9 us -> 23.7 us  [advected(): pl.pallas_call(advect_kernel, out_shape=jax.ShapeDtypeStruct(weighted.sha...]
where the time goes in v1:
time: 95.1 us; the launch traced here: 94.9 us
  Pallas kernels  92.6 us (97%)
  local copies, waits for them, and re-layouts  2.29 us (2%)
    pallas_call x1, Pallas kernels, localized(): pl.pallas_call(localize_kernel, out_shape=jax.ShapeDtypeStruct((kinds, le...  68.9 us
    pallas_call x1, Pallas kernels, advected(): pl.pallas_call(advect_kernel, out_shape=jax.ShapeDtypeStruct(weighted.sha...  23.7 us
    unnamed x7, local copies, waits for them, and re-layouts  2.29 us

profile of v1, /device:TPU:0, one launch (start us, length us, event | category | flops | bytes accessed | tf_op | source)
XLA Modules:
  0.0 94.9 jit_solution(1787772423867887617)
XLA Ops:
  0.0 0.0 copy-start.2
  0.0 0.0 copy-start.1
  0.0 68.9 %localize.1.first = f32[3,3,32,1024]{3,2,1,0:T(8,128)} custom-call(bf16[2,3,32,2048]{3,2,1,0:T(8,128)(2,1)} %control.1, bf16[3,2,3,32,2048]{4,3,2,1,0:T(8,128)(2,1)} %pert.1, bf16[256,2048]{1,0:T(8,128)(2,1)} %taper.1, bf16[32,256]{1,0:T(8,128)(2,1)} %row_part.1), custom_call_target="tpu_custom_call" | custom-call | tf_op jit(solution)/shard_map/localize/pallas_call | solution.py:524
  69.0 0.0 copy-done.2
  69.0 0.0 copy-done.1
  69.0 0.0 copy-start
  69.0 1.3 %copy-done = f32[3,3,32,1024]{3,2,1,0:T(8,128)S(1)} copy-done((f32[3,3,32,1024]{3,2,1,0:T(8,128)S(1)}, f32[3,3,32,1024]{3,2,1,0:T(8,128)}, u32[]{:S(2)}) %copy-start) | copy-done | bytes 1179672
  70.2 23.7 %advect.1 = f32[3,3,32,1024]{3,2,1,0:T(8,128)S(1)} custom-call(f32[3,3,32,1024]{3,2,1,0:T(8,128)S(1)} %copy-done, f32[3,3,32,1024]{3,2,1,0:T(8,128)S(1)} %copy-done.1, f32[2,3,32,1024]{3,2,1,0:T(8,128)S(1)} %copy-done.2), custom_call_target="tpu_custom_call" | custom-call | tf_op jit(solution)/shard_map/advect/pallas_call | solution.py:189
  93.9 1.0 %copy.8 = f32[3,3,32,1024]{3,2,1,0:T(8,128)} copy(f32[3,3,32,1024]{3,2,1,0:T(8,128)S(1)} %advect.1) | data formatting | bytes 2359296
Async XLA Ops:
  0.0 69.0 %copy-start.2 = (f32[2,3,32,1024]{3,2,1,0:T(8,128)S(1)}, f32[2,3,32,1024]{3,2,1,0:T(8,128)}, u32[]{:S(2)}) copy-start(f32[2,3,32,1024]{3,2,1,0:T(8,128)} %slope.1) | copy-start | bytes 2359300
  0.0 69.0 %copy-start.1 = (f32[3,3,32,1024]{3,2,1,0:T(8,128)S(1)}, f32[3,3,32,1024]{3,2,1,0:T(8,128)}, u32[]{:S(2)}) copy-start(f32[3,3,32,1024]{3,2,1,0:T(8,128)} %courant.1) | copy-start | bytes 3538948
  69.0 1.3 %copy-start = (f32[3,3,32,1024]{3,2,1,0:T(8,128)S(1)}, f32[3,3,32,1024]{3,2,1,0:T(8,128)}, u32[]{:S(2)}) copy-start(f32[3,3,32,1024]{3,2,1,0:T(8,128)} %localize.1.first) | copy-start | bytes 3538948

commit v2 on v1

v2 whole, which is shorter than its diff:
```python
import jax
import jax.numpy as jnp
from jax import lax
from jax.experimental import pallas as pl
from jax.experimental.pallas import tpu as pltpu
from jax.sharding import PartitionSpec as P

STEPS = 4


MESH = pl.DeviceIdType.MESH


def kernel(
    control, pert, taper, row_part, courant_in, slope_in, out, own, gathered, row_all, staged, halves,
    taper_all, pert_all, courant, slope, state, factors, level_send, level_halo, row_edge, row_halo,
    column_halo, one_send, one_recv, row_send, row_recv, two_send, two_recv, pass_send, pass_recv,
    pert_send, pert_recv, first_send, first_recv, line_send, line_recv, side_send, side_recv, lev_send,
    lev_recv, up_send, up_recv, edge_send, edge_recv, column_send, column_recv, own_sem,
):
    count, mems, levs = (lax.axis_size(axis) for axis in ("row", "mem", "lev"))
    me, mem_at, lev_at = (lax.axis_index(axis) for axis in ("row", "mem", "lev"))
    kinds, members, levels, rows, columns = pert.shape
    depth, width = taper.shape[0], out.shape[3]
    inner = 2 if count % 2 == 0 else 1
    outer = count // inner
    line_at, side_at = me // inner, me % inner
    share, lanes = depth // levs, width // inner
    sent = []

    def remote(source, landing, to, at, **target):
        return pltpu.make_async_remote_copy(
            src_ref=source, dst_ref=landing, send_sem=to, recv_sem=at, device_id=target,
            device_id_type=MESH,
        )

    def send(there, copy):
        sent.append((there, copy))
        when(there, lambda: copy().start())

    def when(there, action):
        if there is True:
            action()
        else:
            pl.when(there)(action)

    def own_columns(at):
        return pl.ds(pl.multiple_of(at * width, width), width)

    def block(source, at, level):
        if len(source.shape) == 5:
            return source.at[at, :, level]
        return source.at[:, level, :, pl.ds(pl.multiple_of(at * depth, depth), depth)]

    def level_of(turn):
        return jnp.where(lev_at > 0, turn, levels - 1 - turn)

    offsets = sorted(range(1, count), key=lambda by: -min(by // inner, outer - by // inner))

    def peer_of(by):
        return (line_at + by // inner) % outer * inner + (side_at + by % inner) % inner

    def one(peer, slot, level):
        return remote(
            block(own, peer, level), gathered.at[slot, level], one_send.at[peer, level],
            one_recv.at[slot, level], row=peer,
        )

    def row(peer, slot):
        return remote(row_all.at[me], row_all.at[slot], row_send.at[peer], row_recv.at[slot], row=peer)

    def two(peer, slot, level):
        return remote(
            staged.at[peer, level], halves.at[level, slot, mem_at], two_send.at[peer, level],
            two_recv.at[slot, level], row=peer,
        )

    def onward(peer, slot, level, place):
        part = halves.at[level, slot, place]
        return remote(
            part, part, pass_send.at[peer, slot, level], pass_recv.at[place, slot, level], mem=peer
        )

    def pert_copy(peer, slot):
        return remote(
            pert.at[:, :, :, :, own_columns(peer)], pert_all.at[slot], pert_send.at[peer],
            pert_recv.at[slot], mem=peer,
        )

    def piece(origin, lev, side):
        return taper_all.at[
            origin,
            pl.ds(pl.multiple_of(lev * share, share), share),
            pl.ds(pl.multiple_of(side * lanes, lanes), lanes),
        ]

    other = line_at * inner + (inner - 1 - side_at)

    def first(origin, side):
        part = piece(origin, lev_at, side)
        return remote(part, part, first_send.at[0], first_recv.at[0], row=other)

    def side(origin, at):
        part = piece(origin, lev_at, at)
        return remote(part, part, side_send.at[origin], side_recv.at[origin], row=other)

    def line(way, hop, turn, sending):
        back = hop if sending else hop + 1
        from_line = line_at - back if way == 0 else line_at + back
        to_line = line_at + 1 if way == 0 else line_at - 1
        origin = from_line * inner + (side_at if turn == 0 else inner - 1 - side_at)
        there = from_line >= 0 if way == 0 else from_line <= outer - 1
        if sending:
            there = there & (to_line <= outer - 1 if way == 0 else to_line >= 0)

        def copy():
            part = piece(origin, lev_at, side_at)
            return remote(
                part, part, line_send.at[way, hop, turn], line_recv.at[way, hop, turn],
                row=to_line * inner + side_at,
            )

        return origin, there, copy

    def lev_copy(origin, at, shift, sending):
        part = piece(origin, lev_at if sending else (lev_at + levs - shift) % levs, at)
        return remote(
            part, part, lev_send.at[origin, at, shift - 1], lev_recv.at[origin, at, shift - 1],
            lev=(lev_at + shift) % levs,
        )

    def across(there, origin, at):
        for shift in range(1, levs):
            send(there, lambda shift=shift: lev_copy(origin, at, shift, True))

    def along_line(hop, turn):
        if outer == 1:
            return
        for way in range(2):
            _, there, copy = line(way, hop, turn, True)
            send(there, copy)

    def one_chunk(turn):
        level = level_of(turn)
        for by in offsets:
            send(True, lambda by=by: one(peer_of(by), me, level))

    def row_step(turn):
        level = level_of(turn)
        for by in offsets:
            slot = peer_of(by)
            one(slot, slot, level).wait_recv()
        whole = row_all[...].reshape(count * rows, count * rows)
        for member in range(members):
            tapered = jnp.dot(
                whole, gathered[:, level, member].reshape(count * rows, depth),
                preferred_element_type=jnp.float32,
            )
            staged[:, level, member] = tapered.astype(jnp.bfloat16).reshape(count, rows, depth)
        for by in offsets:
            send(True, lambda by=by: two(peer_of(by), me, level))
        for member in range(members):
            halves[level, me, mem_at, member] = staged[me, level, member]
        for shift in range(1, mems):
            send(True, lambda shift=shift: onward((mem_at + shift) % mems, me, level, mem_at))

    def set_factors():
        row_at = lax.broadcasted_iota(jnp.int32, (rows, width), 0)
        column_at = lax.broadcasted_iota(jnp.int32, (rows, width), 1)
        for turn in range(levels):
            level = level_of(turn)
            centre = jnp.ones((rows, width), jnp.float32)
            for at in range(3):
                speed = courant[at, level]
                ahead, back = jnp.maximum(speed, 0.0), -jnp.minimum(speed, 0.0)
                centre = centre - ahead - back
                if at == 0:
                    ahead, back = jnp.where(lev_at > 0, ahead, back), jnp.where(lev_at > 0, back, ahead)
                if at == 1:
                    ahead = jnp.where(row_at == 0, 0.0, ahead)
                    back = jnp.where(row_at == rows - 1, 0.0, back)
                if at == 2:
                    ahead = jnp.where(column_at == 0, 0.0, ahead)
                    back = jnp.where(column_at == width - 1, 0.0, back)
                factors[1 + 2 * at, turn] = ahead
                factors[2 + 2 * at, turn] = back
            factors[0, turn] = centre

    neighbours = []
    if count > 1:
        neighbours += [("row", 0, me > 0, me - 1), ("row", 1, me < count - 1, me + 1)]
    if mems > 1:
        neighbours += [("mem", 0, mem_at > 0, mem_at - 1), ("mem", 1, mem_at < mems - 1, mem_at + 1)]

    def part_of(turn):
        return min(turn, 1)

    def turns_of(part):
        return range(0, 1) if part == 0 else range(1, levels)

    parts = 1 if levels == 1 else 2

    def edge_copy(step, kind, part, axis, at, target, arriving):
        turns = pl.ds(0, 1) if part == 0 else pl.ds(1, levels - 1)
        landed = at if arriving else 1 - at
        if axis == "row":
            source = row_edge.at[step, at, kind, turns]
            landing = row_halo.at[step, landed, kind, turns]
            to, there = edge_send.at[step, at, kind, part], edge_recv.at[step, landed, kind, part]
        else:
            source = state.at[step, kind, turns, :, pl.ds(0 if at == 0 else width - 128, 128)]
            landing = column_halo.at[step, landed, kind, turns]
            to, there = column_send.at[step, at, kind, part], column_recv.at[step, landed, kind, part]
        return remote(landing if arriving else source, landing, to, there, **{axis: target})

    def level_copy(step, kind):
        return remote(
            level_send.at[step, kind], level_halo.at[step, kind], up_send.at[step, kind],
            up_recv.at[step, kind], lev=levs - 1 - lev_at,
        )

    def send_edges(step, kind, part):
        for axis, at, there, target in neighbours:

            @pl.when(there)
            def _():
                if axis == "row":
                    for turn in turns_of(part):
                        row_edge[step, at, kind, turn] = state[
                            step, kind, turn, pl.ds(0 if at == 0 else rows - 1, 1)
                        ]
                edge_copy(step, kind, part, axis, at, target, False).start()

    def inside(step, kind, turn, target):
        here = state[step, kind, turn]
        new = here * factors[0, turn]
        new = new + factors[3, turn] * pltpu.roll(here, 1, 0)
        new = new + factors[4, turn] * pltpu.roll(here, rows - 1, 0)
        new = new + factors[5, turn] * pltpu.roll(here, 1, 1)
        new = new + factors[6, turn] * pltpu.roll(here, width - 1, 1)
        if turn > 0:
            new = new + factors[1, turn] * state[step, kind, turn - 1]
        if turn < levels - 1:
            new = new + factors[2, turn] * state[step, kind, turn + 1]
        if kind == 2:
            level = level_of(turn)
            new = new - (
                state[step, 0, turn] * slope[0, level] + state[step, 1, turn] * slope[1, level]
            )
        target[...] = new

    def take_edges(step, kind, part, view):
        lane_at = lax.broadcasted_iota(jnp.int32, (rows, 128), 1)
        for axis, at, there, target in neighbours:

            @pl.when(there)
            def _():
                edge_copy(step, kind, part, axis, at, target, True).wait_recv()
                for turn in turns_of(part):
                    level, new = level_of(turn), view(kind, turn)
                    if axis == "row":
                        edge = pl.ds(0 if at == 0 else rows - 1, 1)
                        speed = courant[1, level, edge]
                        speed = -jnp.minimum(speed, 0.0) if at else jnp.maximum(speed, 0.0)
                        new[edge] = new[edge] + speed * row_halo[step, at, kind, turn]
                    else:
                        columns_at = pl.ds(width - 128 if at else 0, 128)
                        speed = courant[2, level, :, columns_at]
                        speed = -jnp.minimum(speed, 0.0) if at else jnp.maximum(speed, 0.0)
                        beside = pltpu.roll(column_halo[step, at, kind, turn], 127 if at else 1, 1)
                        new[:, columns_at] = new[:, columns_at] + jnp.where(
                            lane_at == (127 if at else 0), speed * beside, 0.0
                        )

    def one_step(step, view, last):
        for kind in range(kinds):
            inside(step, kind, 0, view(kind, 0))
            take_edges(step, kind, 0, view)
            if levs > 1:
                level_copy(step, kind).wait_recv()
                new = view(kind, 0)
                whole = new[...] + factors[1, 0] * level_halo[step, kind].astype(jnp.float32)
                new[...] = whole
                if not last:
                    level_send[step + 1, kind] = whole.astype(level_send.dtype)
                    level_copy(step + 1, kind).start()
            if not last:
                send_edges(step + 1, kind, 0)
        for kind in range(kinds):
            for turn in turns_of(1):
                inside(step, kind, turn, view(kind, turn))
            if parts > 1:
                take_edges(step, kind, 1, view)
                if not last:
                    send_edges(step + 1, kind, 1)

    barrier = pltpu.get_barrier_semaphore()
    for axis, here, size in (("row", me, count), ("mem", mem_at, mems), ("lev", lev_at, levs)):

        @pl.loop(1, size)
        def _(shift):
            pl.semaphore_signal(
                barrier, inc=1, device_id={axis: (here + shift) % size}, device_id_type=MESH
            )

    fetches = [
        pltpu.make_async_copy(taper.at[:, own_columns(mem_at)], taper_all.at[me], own_sem.at[0]),
        pltpu.make_async_copy(control, own, own_sem.at[1]),
        pltpu.make_async_copy(row_part, row_all.at[me], own_sem.at[2]),
        pltpu.make_async_copy(
            pert.at[:, :, :, :, own_columns(mem_at)], pert_all.at[mem_at], own_sem.at[3]
        ),
    ]
    late = [
        pltpu.make_async_copy(courant_in, courant, own_sem.at[4 + levels]),
        pltpu.make_async_copy(slope_in, slope, own_sem.at[5 + levels]),
    ]
    for level in range(levels):
        fetches.append(
            pltpu.make_async_copy(
                block(control, me, level), gathered.at[me, level], own_sem.at[4 + level]
            )
        )
    for fetch in fetches + late:
        fetch.start()
    for fetch in fetches[:3]:
        fetch.wait()
    pl.semaphore_wait(barrier, count + mems + levs - 3)

    if inner > 1:
        send(True, lambda: first(me, inner - 1 - side_at))
    along_line(0, 0)
    if inner > 1:
        send(True, lambda: side(me, side_at))
    for by in offsets:
        send(True, lambda by=by: row(peer_of(by), me))
    one_chunk(0)
    for shift in range(1, mems):
        send(True, lambda shift=shift: pert_copy((mem_at + shift) % mems, mem_at))
    for fetch in fetches[3:] + late:
        fetch.wait()
    set_factors()
    if inner > 1:
        first(other, side_at).wait_recv()
        along_line(0, 1)
        across(True, other, side_at)
    for turn in range(1, levels - 1):
        one_chunk(turn)
    if inner > 1:
        side(other, inner - 1 - side_at).wait_recv()
        across(True, other, inner - 1 - side_at)

    def hop_step(hop):
        for turn in range(inner):
            for way in range(2):
                origin, there, copy = line(way, hop, turn, False)

                def arrived(copy=copy):
                    copy().wait_recv()

                when(there, arrived)
                if hop + 1 < outer - 1:
                    _, onwards, relay = line(way, hop + 1, turn, True)
                    send(onwards, relay)
                if inner > 1:
                    send(there, lambda origin=origin: side(origin, side_at))
                across(there, origin, side_at)

    def side_step(hop):
        for turn in range(inner):
            for way in range(2):
                origin, there, _ = line(way, hop, turn, False)
                if inner > 1:

                    def arrived(origin=origin):
                        side(origin, inner - 1 - side_at).wait_recv()

                    when(there, arrived)
                    across(there, origin, inner - 1 - side_at)

    ready = 0
    for hop in range(outer - 1):
        hop_step(hop)
        if hop == 0:
            one_chunk(levels - 1)
            for by in offsets:
                slot = peer_of(by)
                row(slot, slot).wait_recv()
        if ready < levels:
            row_step(ready)
            ready += 1
        side_step(hop)
    for turn in range(ready, levels):
        row_step(turn)

    for turn in range(levels):
        level = level_of(turn)
        for by in offsets:
            slot = peer_of(by)
            two(slot, slot, level).wait_recv()
            for shift in range(1, mems):
                send(
                    True,
                    lambda shift=shift, slot=slot, level=level: onward(
                        (mem_at + shift) % mems, slot, level, mem_at
                    ),
                )

    for by in offsets:
        origin = peer_of(by)
        for at in range(inner):
            for shift in range(1, levs):
                lev_copy(origin, at, shift, False).wait_recv()
    for shift in range(1, mems):
        peer = (mem_at + shift) % mems
        pert_copy(peer, peer).wait_recv()

    span = min(width, 256)
    for turn in range(levels):
        level = level_of(turn)
        for shift in range(1, mems):
            peer = (mem_at + shift) % mems

            @pl.loop(0, count)
            def _(slot):
                onward(peer, slot, level, peer).wait_recv()

        for start in range(0, width, span):
            total = jnp.zeros((mems * members * rows, span), jnp.float32)
            for slot in range(count):
                total = total + jnp.dot(
                    halves[level, slot].reshape(mems * members * rows, depth),
                    taper_all[slot, :, pl.ds(start, span)],
                    preferred_element_type=jnp.float32,
                )
            for kind in range(kinds):
                weighted = jnp.zeros((rows, span), jnp.float32)
                for mem in range(mems):
                    for member in range(members):
                        at = (mem * members + member) * rows
                        weighted = weighted + pert_all[
                            mem, kind, member, level, :, pl.ds(start, span)
                        ].astype(jnp.float32) * total[at : at + rows]
                state[0, kind, turn, :, pl.ds(start, span)] = weighted
                if turn == 0 and levs > 1:
                    level_send[0, kind, :, pl.ds(start, span)] = weighted.astype(level_send.dtype)
        if turn == 0:
            for kind in range(kinds):
                if levs > 1:
                    level_copy(0, kind).start()
                send_edges(0, kind, 0)
    if parts > 1:
        for kind in range(kinds):
            send_edges(0, kind, 1)

    @pl.loop(0, STEPS - 1)
    def _(step):
        one_step(step, lambda kind, turn: state.at[step + 1, kind, turn], False)

    one_step(STEPS - 1, lambda kind, turn: out.at[kind, level_of(turn)], True)

    for there, copy in sent:
        when(there, lambda copy=copy: copy().wait_send())

    @pl.loop(0, STEPS)
    def _(step):
        for kind in range(kinds):
            if levs > 1:
                level_copy(step, kind).wait_send()
            for part in range(parts):
                for axis, at, there, target in neighbours:

                    @pl.when(there)
                    def _():
                        edge_copy(step, kind, part, axis, at, target, False).wait_send()


def on_device(
    control_fields, perturbations, column_taper, row_taper, courant_numbers, tracer_slope
):
    members, levels, rows, columns = control_fields.shape
    kinds = perturbations.shape[0]
    count, mems, levs = (lax.axis_size(axis) for axis in ("row", "mem", "lev"))
    depth, width = columns // count, columns // mems
    if depth % 128:
        control_fields = control_fields.reshape(members, levels, rows, count, depth)
        control_fields = control_fields.transpose(3, 0, 1, 2, 4)
    low, full, dma = jnp.bfloat16, jnp.float32, pltpu.SemaphoreType.DMA
    pairs = [dma((count, levels))] * 2 + [dma((count,))] * 2 + [dma((count, levels))] * 2
    pairs += [dma((mems, count, levels))] * 2 + [dma((mems,))] * 2 + [dma((1,))] * 2
    pairs += [dma((2, count, 2))] * 2 + [dma((count,))] * 2 + [dma((count, 2, levs))] * 2
    pairs += [dma((STEPS, kinds))] * 2 + [dma((STEPS, 2, kinds, 2))] * 4
    return pl.pallas_call(
        kernel,
        out_shape=jax.ShapeDtypeStruct((kinds, levels, rows, width), full),
        in_specs=[pl.BlockSpec(memory_space=pltpu.HBM)] * 6,
        out_specs=pl.BlockSpec(memory_space=pltpu.VMEM),
        scratch_shapes=[
            pltpu.VMEM(control_fields.shape, low),
            pltpu.VMEM((count, levels, members, rows, depth), low),
            pltpu.VMEM((count, rows, count * rows), low),
            pltpu.VMEM((count, levels, members, rows, depth), low),
            pltpu.VMEM((levels, count, mems, members, rows, depth), low),
            pltpu.VMEM((count, depth, width), low),
            pltpu.VMEM((mems, kinds, members, levels, rows, width), low),
            pltpu.VMEM(courant_numbers.shape, full),
            pltpu.VMEM(tracer_slope.shape, full),
            pltpu.VMEM((STEPS, kinds, levels, rows, width), full),
            pltpu.VMEM((7, levels, rows, width), full),
            pltpu.VMEM((STEPS, kinds, rows, width), low),
            pltpu.VMEM((STEPS, kinds, rows, width), low),
            pltpu.VMEM((STEPS, 2, kinds, levels, 1, width), full),
            pltpu.VMEM((STEPS, 2, kinds, levels, 1, width), full),
            pltpu.VMEM((STEPS, 2, kinds, levels, rows, 128), full),
            *pairs,
            dma((6 + levels,)),
        ],
        compiler_params=pltpu.CompilerParams(
            collective_id=0, has_side_effects=True, vmem_limit_bytes=44 << 20
        ),
        name="increment",
    )(
        *(
            pltpu.with_memory_space_constraint(operand, pltpu.HBM)
            for operand in (
                control_fields, perturbations, column_taper, row_taper, courant_numbers, tracer_slope
            )
        )
    )


def solution(mesh):
    assert mesh.shape["lev"] <= 2
    placed = (
        P("mem", "lev", "row", None),
        P(None, "mem", "lev", "row", None),
        P("row", None),
        P("row", None),
        P(None, "lev", "row", "mem"),
        P(None, "lev", "row", "mem"),
    )
    return jax.shard_map(
        on_device,
        mesh=mesh,
        in_specs=placed,
        out_specs=P(None, "lev", "row", "mem"),
        check_vma=False,
    )
```

time: 95.1 us -> 88.7 us (0.933)
  Pallas kernels: 92.6 us -> 87.5 us
  local copies, waits for them, and re-layouts: 2.29 us -> 1.02 us
    pallas_call x2 -> x1, Pallas kernels: 92.6 us -> 87.5 us  [on_device(): pl.pallas_call(kernel, out_shape=jax.ShapeDtypeStruct((kinds, levels, row...]
    unnamed x7 -> x1, local copies, waits for them, and re-layouts: 2.29 us -> 1.02 us
where the time goes in v2:
time: 88.7 us; the launch traced here: 88.6 us
  Pallas kernels  87.5 us (99%)
  local copies, waits for them, and re-layouts  1.02 us (1%)
    pallas_call x1, Pallas kernels, on_device(): pl.pallas_call(kernel, out_shape=jax.ShapeDtypeStruct((kinds, levels, row...  87.5 us

profile of v2, /device:TPU:0, one launch (start us, length us, event | category | flops | bytes accessed | tf_op | source)
XLA Modules:
  0.0 88.6 jit_solution(13217844364448973527)
XLA Ops:
  0.0 87.5 %increment.1 = f32[3,3,32,1024]{3,2,1,0:T(8,128)S(1)} custom-call(bf16[2,3,32,2048]{3,2,1,0:T(8,128)(2,1)} %control.1, bf16[3,2,3,32,2048]{4,3,2,1,0:T(8,128)(2,1)} %pert.1, bf16[256,2048]{1,0:T(8,128)(2,1)} %taper.1, bf16[32,256]{1,0:T(8,128)(2,1)} %row_part.1, f32[3,3,32,1024]{3,2,1,0:T(8,128)} %courant_in.1, f32[2,3,32,1024]{3,2,1,0:T(8,128)} %slope_in.1), custom_call_target="tpu_custom_call" | custom-call | tf_op jit(solution)/shard_map/increment/pallas_call | solution.py:493
  87.6 1.0 %copy.8 = f32[3,3,32,1024]{3,2,1,0:T(8,128)} copy(f32[3,3,32,1024]{3,2,1,0:T(8,128)S(1)} %increment.1) | data formatting | bytes 2359296

commit v3 on v2

--- a/solution.py
+++ b/solution.py
@@ -26,7 +26,7 @@
     outer = count // inner
     line_at, side_at = me // inner, me % inner
     share, lanes = depth // levs, width // inner
-    sent = []
+    early = []
 
     def remote(source, landing, to, at, **target):
         return pltpu.make_async_remote_copy(
@@ -34,9 +34,12 @@
             device_id_type=MESH,
         )
 
+    def start(there, copy):
+        when(there, lambda: copy().start())
+
     def send(there, copy):
-        sent.append((there, copy))
-        when(there, lambda: copy().start())
+        early.append((there, copy))
+        start(there, copy)
 
     def when(there, action):
         if there is True:
@@ -62,24 +65,46 @@
 
     def one(peer, slot, level):
         return remote(
-            block(own, peer, level), gathered.at[slot, level], one_send.at[peer, level],
-            one_recv.at[slot, level], row=peer,
+            block(own, peer, level), gathered.at[slot, level], one_send.at[0],
+            one_recv.at[level], row=peer,
         )
 
     def row(peer, slot):
-        return remote(row_all.at[me], row_all.at[slot], row_send.at[peer], row_recv.at[slot], row=peer)
+        return remote(row_all.at[me], row_all.at[slot], row_send.at[0], row_recv.at[0], row=peer)
 
     def two(peer, slot, level):
         return remote(
-            staged.at[peer, level], halves.at[level, slot, mem_at], two_send.at[peer, level],
-            two_recv.at[slot, level], row=peer,
+            staged.at[peer, level], halves.at[level, slot, mem_at], two_send.at[0],
+            two_recv.at[level], row=peer,
         )
 
-    def onward(peer, slot, level, place):
-        part = halves.at[level, slot, place]
-        return remote(
-            part, part, pass_send.at[peer, slot, level], pass_recv.at[place, slot, level], mem=peer
-        )
+    def onward(peer, level, place):
+        part = halves.at[level, :, place]
+        return remote(part, part, pass_send.at[peer, level], pass_recv.at[place, level], mem=peer)
+
+    def all_one(level):
+        part = gathered.at[pl.ds(0, count - 1), level]
+        return remote(part, part, one_send.at[0], one_recv.at[level], row=peer_of(1))
+
+    def all_row():
+        part = row_all.at[pl.ds(0, count - 1)]
+        return remote(part, part, row_send.at[0], row_recv.at[0], row=peer_of(1))
+
+    def all_two(level):
+        part = gathered.at[pl.ds(0, count - 1), level]
+        return remote(part, part, two_send.at[0], two_recv.at[level], row=peer_of(1))
+
+    def all_sent(to):
+        part = gathered.at[pl.ds(0, count - 1)]
+        return remote(part, part, to, two_recv.at[0], row=peer_of(1))
+
+    def all_side():
+        part = taper_all.at[pl.ds(0, count - 1), pl.ds(0, share), pl.ds(0, lanes)]
+        return remote(part, part, side_send.at[0], side_recv.at[0], row=peer_of(1))
+
+    def all_lev():
+        part = taper_all.at[pl.ds(0, count - 1), pl.ds(0, share)]
+        return remote(part, part, lev_send.at[0], lev_recv.at[0], lev=levs - 1 - lev_at)
 
     def pert_copy(peer, slot):
         return remote(
@@ -102,7 +127,7 @@
 
     def side(origin, at):
         part = piece(origin, lev_at, at)
-        return remote(part, part, side_send.at[origin], side_recv.at[origin], row=other)
+        return remote(part, part, side_send.at[0], side_recv.at[origin], row=other)
 
     def line(way, hop, turn, sending):
         back = hop if sending else hop + 1
@@ -122,16 +147,13 @@
 
         return origin, there, copy
 
-    def lev_copy(origin, at, shift, sending):
-        part = piece(origin, lev_at if sending else (lev_at + levs - shift) % levs, at)
-        return remote(
-            part, part, lev_send.at[origin, at, shift - 1], lev_recv.at[origin, at, shift - 1],
-            lev=(lev_at + shift) % levs,
-        )
-
     def across(there, origin, at):
-        for shift in range(1, levs):
-            send(there, lambda shift=shift: lev_copy(origin, at, shift, True))
+        def copy():
+            part = piece(origin, lev_at, at)
+            return remote(part, part, lev_send.at[0], lev_recv.at[0], lev=levs - 1 - lev_at)
+
+        if levs > 1:
+            start(there, copy)
 
     def along_line(hop, turn):
         if outer == 1:
@@ -140,16 +162,17 @@
             _, there, copy = line(way, hop, turn, True)
             send(there, copy)
 
-    def one_chunk(turn):
+    def one_chunk(turn, half=None):
         level = level_of(turn)
-        for by in offsets:
-            send(True, lambda by=by: one(peer_of(by), me, level))
+        cut = (len(offsets) + 1) // 2
+        part = offsets if half is None else offsets[:cut] if half == 0 else offsets[cut:]
+        for by in part:
+            start(True, lambda by=by: one(peer_of(by), me, level))
 
     def row_step(turn):
         level = level_of(turn)
-        for by in offsets:
-            slot = peer_of(by)
-            one(slot, slot, level).wait_recv()
+        if count > 1:
+            all_one(level).wait_recv()
         whole = row_all[...].reshape(count * rows, count * rows)
         for member in range(members):
             tapered = jnp.dot(
@@ -158,11 +181,9 @@
             )
             staged[:, level, member] = tapered.astype(jnp.bfloat16).reshape(count, rows, depth)
         for by in offsets:
-            send(True, lambda by=by: two(peer_of(by), me, level))
+            start(True, lambda by=by: two(peer_of(by), me, level))
         for member in range(members):
             halves[level, me, mem_at, member] = staged[me, level, member]
-        for shift in range(1, mems):
-            send(True, lambda shift=shift: onward((mem_at + shift) % mems, me, level, mem_at))
 
     def set_factors():
         row_at = lax.broadcasted_iota(jnp.int32, (rows, width), 0)
@@ -201,22 +222,23 @@
     parts = 1 if levels == 1 else 2
 
     def edge_copy(step, kind, part, axis, at, target, arriving):
-        turns = pl.ds(0, 1) if part == 0 else pl.ds(1, levels - 1)
-        landed = at if arriving else 1 - at
+        at_kind, turns = (kind, pl.ds(0, 1)) if part == 0 else (pl.ds(0, kinds), pl.ds(1, levels - 1))
+        landed, slot = at if arriving else 1 - at, kind if part == 0 else kinds
         if axis == "row":
-            source = row_edge.at[step, at, kind, turns]
-            landing = row_halo.at[step, landed, kind, turns]
-            to, there = edge_send.at[step, at, kind, part], edge_recv.at[step, landed, kind, part]
+            source = row_edge.at[step, at, at_kind, turns]
+            landing = row_halo.at[step, landed, at_kind, turns]
+            to, there = edge_send.at[step, at], edge_recv.at[step % 2, landed, slot]
         else:
-            source = state.at[step, kind, turns, :, pl.ds(0 if at == 0 else width - 128, 128)]
-            landing = column_halo.at[step, landed, kind, turns]
-            to, there = column_send.at[step, at, kind, part], column_recv.at[step, landed, kind, part]
+            source = state.at[step, at_kind, turns, :, pl.ds(0 if at == 0 else width - 128, 128)]
+            landing = column_halo.at[step, landed, at_kind, turns]
+            place = column_recv.shape[1]
+            to, there = column_send.at[step, at % place], column_recv.at[step % 2, landed % place, slot]
         return remote(landing if arriving else source, landing, to, there, **{axis: target})
 
     def level_copy(step, kind):
         return remote(
-            level_send.at[step, kind], level_halo.at[step, kind], up_send.at[step, kind],
-            up_recv.at[step, kind], lev=levs - 1 - lev_at,
+            level_send.at[step, kind], level_halo.at[step, kind], up_send.at[step],
+            up_recv.at[step % 2, kind], lev=levs - 1 - lev_at,
         )
 
     def send_edges(step, kind, part):
@@ -225,11 +247,27 @@
             @pl.when(there)
             def _():
                 if axis == "row":
-                    for turn in turns_of(part):
-                        row_edge[step, at, kind, turn] = state[
-                            step, kind, turn, pl.ds(0 if at == 0 else rows - 1, 1)
-                        ]
+                    for variable in [kind] if part == 0 else range(kinds):
+                        for turn in turns_of(part):
+                            row_edge[step, at, variable, turn] = state[
+                                step, variable, turn, pl.ds(0 if at == 0 else rows - 1, 1)
+                            ]
                 edge_copy(step, kind, part, axis, at, target, False).start()
+
+    def settle_step(step):
+        if levs > 1:
+            remote(
+                level_send.at[step], level_send.at[step], up_send.at[step], up_recv.at[step % 2, 0],
+                lev=levs - 1 - lev_at,
+            ).wait_send()
+        for axis, at, there, target in neighbours:
+
+            @pl.when(there)
+            def _():
+                part = (row_edge if axis == "row" else column_halo).at[step, at]
+                place = at % column_recv.shape[1]
+                to = edge_send.at[step, at] if axis == "row" else column_send.at[step, place]
+                remote(part, part, to, edge_recv.at[0, 0, 0], **{axis: target}).wait_send()
 
     def inside(step, kind, turn, target):
         here = state[step, kind, turn]
@@ -256,18 +294,21 @@
             @pl.when(there)
             def _():
                 edge_copy(step, kind, part, axis, at, target, True).wait_recv()
-                for turn in turns_of(part):
-                    level, new = level_of(turn), view(kind, turn)
+                whole = [kind] if part == 0 else range(kinds)
+                for kind_at, turn in [(k, t) for k in whole for t in turns_of(part)]:
+                    level, new = level_of(turn), view(kind_at, turn)
                     if axis == "row":
                         edge = pl.ds(0 if at == 0 else rows - 1, 1)
                         speed = courant[1, level, edge]
                         speed = -jnp.minimum(speed, 0.0) if at else jnp.maximum(speed, 0.0)
-                        new[edge] = new[edge] + speed * row_halo[step, at, kind, turn]
+                        new[edge] = new[edge] + speed * row_halo[step, at, kind_at, turn]
                     else:
                         columns_at = pl.ds(width - 128 if at else 0, 128)
                         speed = courant[2, level, :, columns_at]
                         speed = -jnp.minimum(speed, 0.0) if at else jnp.maximum(speed, 0.0)
-                        beside = pltpu.roll(column_halo[step, at, kind, turn], 127 if at else 1, 1)
+                        beside = pltpu.roll(
+                            column_halo[step, at, kind_at, turn], 127 if at else 1, 1
+                        )
                         new[:, columns_at] = new[:, columns_at] + jnp.where(
                             lane_at == (127 if at else 0), speed * beside, 0.0
                         )
@@ -275,6 +316,9 @@
     def one_step(step, view, last):
         for kind in range(kinds):
             inside(step, kind, 0, view(kind, 0))
+        for kind in range(kinds):
+            for turn in turns_of(1):
+                inside(step, kind, turn, view(kind, turn))
             take_edges(step, kind, 0, view)
             if levs > 1:
                 level_copy(step, kind).wait_recv()
@@ -286,13 +330,11 @@
                     level_copy(step + 1, kind).start()
             if not last:
                 send_edges(step + 1, kind, 0)
-        for kind in range(kinds):
-            for turn in turns_of(1):
-                inside(step, kind, turn, view(kind, turn))
-            if parts > 1:
-                take_edges(step, kind, 1, view)
-                if not last:
-                    send_edges(step + 1, kind, 1)
+        if parts > 1:
+            take_edges(step, 0, 1, view)
+            if not last:
+                send_edges(step + 1, 0, 1)
+        settle_step(step)
 
     barrier = pltpu.get_barrier_semaphore()
     for axis, here, size in (("row", me, count), ("mem", mem_at, mems), ("lev", lev_at, levs)):
@@ -331,40 +373,30 @@
         send(True, lambda: first(me, inner - 1 - side_at))
     along_line(0, 0)
     if inner > 1:
-        send(True, lambda: side(me, side_at))
+        start(True, lambda: side(me, side_at))
     for by in offsets:
-        send(True, lambda by=by: row(peer_of(by), me))
+        start(True, lambda by=by: row(peer_of(by), me))
     one_chunk(0)
     for shift in range(1, mems):
         send(True, lambda shift=shift: pert_copy((mem_at + shift) % mems, mem_at))
     for fetch in fetches[3:] + late:
         fetch.wait()
     set_factors()
-    if inner > 1:
-        first(other, side_at).wait_recv()
-        along_line(0, 1)
-        across(True, other, side_at)
-    for turn in range(1, levels - 1):
-        one_chunk(turn)
-    if inner > 1:
-        side(other, inner - 1 - side_at).wait_recv()
-        across(True, other, inner - 1 - side_at)
-
-    def hop_step(hop):
-        for turn in range(inner):
-            for way in range(2):
-                origin, there, copy = line(way, hop, turn, False)
-
-                def arrived(copy=copy):
-                    copy().wait_recv()
-
-                when(there, arrived)
-                if hop + 1 < outer - 1:
-                    _, onwards, relay = line(way, hop + 1, turn, True)
-                    send(onwards, relay)
-                if inner > 1:
-                    send(there, lambda origin=origin: side(origin, side_at))
-                across(there, origin, side_at)
+
+    def hop_step(hop, turn):
+        for way in range(2):
+            origin, there, copy = line(way, hop, turn, False)
+
+            def arrived(copy=copy):
+                copy().wait_recv()
+
+            when(there, arrived)
+            if hop + 1 < outer - 1:
+                _, onwards, relay = line(way, hop + 1, turn, True)
+                send(onwards, relay)
+            if inner > 1:
+                start(there, lambda origin=origin: side(origin, side_at))
+            across(there, origin, side_at)
 
     def side_step(hop):
         for turn in range(inner):
@@ -378,52 +410,14 @@
                     when(there, arrived)
                     across(there, origin, inner - 1 - side_at)
 
-    ready = 0
-    for hop in range(outer - 1):
-        hop_step(hop)
-        if hop == 0:
-            one_chunk(levels - 1)
-            for by in offsets:
-                slot = peer_of(by)
-                row(slot, slot).wait_recv()
-        if ready < levels:
-            row_step(ready)
-            ready += 1
-        side_step(hop)
-    for turn in range(ready, levels):
-        row_step(turn)
-
-    for turn in range(levels):
-        level = level_of(turn)
-        for by in offsets:
-            slot = peer_of(by)
-            two(slot, slot, level).wait_recv()
-            for shift in range(1, mems):
-                send(
-                    True,
-                    lambda shift=shift, slot=slot, level=level: onward(
-                        (mem_at + shift) % mems, slot, level, mem_at
-                    ),
-                )
-
-    for by in offsets:
-        origin = peer_of(by)
-        for at in range(inner):
-            for shift in range(1, levs):
-                lev_copy(origin, at, shift, False).wait_recv()
-    for shift in range(1, mems):
-        peer = (mem_at + shift) % mems
-        pert_copy(peer, peer).wait_recv()
-
     span = min(width, 256)
-    for turn in range(levels):
+
+    def product_step(turn):
         level = level_of(turn)
         for shift in range(1, mems):
             peer = (mem_at + shift) % mems
 
-            @pl.loop(0, count)
-            def _(slot):
-                onward(peer, slot, level, peer).wait_recv()
+            onward(peer, level, peer).wait_recv()
 
         for start in range(0, width, span):
             total = jnp.zeros((mems * members * rows, span), jnp.float32)
@@ -449,30 +443,94 @@
                 if levs > 1:
                     level_copy(0, kind).start()
                 send_edges(0, kind, 0)
+
+    def first_step():
+        if inner > 1:
+            first(other, side_at).wait_recv()
+            along_line(0, 1)
+            across(True, other, side_at)
+
+    def other_step():
+        if inner > 1:
+            side(other, inner - 1 - side_at).wait_recv()
+            across(True, other, inner - 1 - side_at)
+
+    def whole_row():
+        if count > 1:
+            all_row().wait_recv()
+
+    def back_step(turn):
+        level = level_of(turn)
+        if count > 1:
+            all_two(level).wait_recv()
+        for shift in range(1, mems):
+            onward((mem_at + shift) % mems, level, mem_at).start()
+
+    def taper_whole():
+        for there, copy in early:
+            when(there, lambda copy=copy: copy().wait_send())
+        if count > 1:
+            all_row().wait_send()
+            all_sent(one_send.at[0]).wait_send()
+            if inner > 1:
+                all_side().wait_send()
+            if levs > 1:
+                all_lev().wait_recv()
+        for shift in range(1, mems):
+            peer = (mem_at + shift) % mems
+            pert_copy(peer, peer).wait_recv()
+
+    def settle():
+        if count > 1:
+            all_sent(two_send.at[0]).wait_send()
+            if levs > 1:
+                all_lev().wait_send()
+        for level in range(levels):
+            for shift in range(1, mems):
+                onward((mem_at + shift) % mems, level, mem_at).wait_send()
+
+    first_step()
+    chunks = [(turn, half) for turn in range(1, levels) for half in range(2)]
+    turns_left, rows_known = list(range(levels)), False
+    for hop in range(outer - 1):
+        for turn in range(inner):
+            hop_step(hop, turn)
+            if chunks:
+                one_chunk(*chunks.pop(0))
+            if hop == 0 and turn == 0:
+                other_step()
+        if hop > 0 and not chunks and turns_left:
+            if not rows_known:
+                whole_row()
+                rows_known = True
+            row_step(turns_left.pop(0))
+        side_step(hop)
+        if 0 < hop < outer - 2 and rows_known and turns_left:
+            row_step(turns_left.pop(0))
+    if outer == 1:
+        other_step()
+    for turn, half in chunks:
+        one_chunk(turn, half)
+    if not rows_known:
+        whole_row()
+    for turn in turns_left:
+        row_step(turn)
+    for turn in range(levels - 1):
+        back_step(turn)
+    taper_whole()
+    for turn in range(levels - 1):
+        product_step(turn)
+    back_step(levels - 1)
+    product_step(levels - 1)
     if parts > 1:
-        for kind in range(kinds):
-            send_edges(0, kind, 1)
+        send_edges(0, 0, 1)
+    settle()
 
     @pl.loop(0, STEPS - 1)
     def _(step):
         one_step(step, lambda kind, turn: state.at[step + 1, kind, turn], False)
 
     one_step(STEPS - 1, lambda kind, turn: out.at[kind, level_of(turn)], True)
-
-    for there, copy in sent:
-        when(there, lambda copy=copy: copy().wait_send())
-
-    @pl.loop(0, STEPS)
-    def _(step):
-        for kind in range(kinds):
-            if levs > 1:
-                level_copy(step, kind).wait_send()
-            for part in range(parts):
-                for axis, at, there, target in neighbours:
-
-                    @pl.when(there)
-                    def _():
-                        edge_copy(step, kind, part, axis, at, target, False).wait_send()
 
 
 def on_device(
@@ -486,10 +544,13 @@
         control_fields = control_fields.reshape(members, levels, rows, count, depth)
         control_fields = control_fields.transpose(3, 0, 1, 2, 4)
     low, full, dma = jnp.bfloat16, jnp.float32, pltpu.SemaphoreType.DMA
-    pairs = [dma((count, levels))] * 2 + [dma((count,))] * 2 + [dma((count, levels))] * 2
-    pairs += [dma((mems, count, levels))] * 2 + [dma((mems,))] * 2 + [dma((1,))] * 2
-    pairs += [dma((2, count, 2))] * 2 + [dma((count,))] * 2 + [dma((count, 2, levs))] * 2
-    pairs += [dma((STEPS, kinds))] * 2 + [dma((STEPS, 2, kinds, 2))] * 4
+    inner = 2 if count % 2 == 0 else 1
+    sides, hops = max(1, min(2, mems - 1)), max(1, count // inner - 1)
+    semaphores = [dma((1,)), dma((levels,)), dma((1,)), dma((1,)), dma((1,)), dma((levels,))]
+    semaphores += [dma((mems, levels))] * 2 + [dma((mems,))] * 2 + [dma((1,))] * 2
+    semaphores += [dma((2, hops, inner))] * 2 + [dma((1,)), dma((count,)), dma((1,)), dma((1,))]
+    semaphores += [dma((STEPS,)), dma((2, kinds)), dma((STEPS, 2)), dma((2, 2, kinds + 1))]
+    semaphores += [dma((STEPS, sides)), dma((2, sides, kinds + 1))]
     return pl.pallas_call(
         kernel,
         out_shape=jax.ShapeDtypeStruct((kinds, levels, rows, width), full),
@@ -512,7 +573,7 @@
             pltpu.VMEM((STEPS, 2, kinds, levels, 1, width), full),
             pltpu.VMEM((STEPS, 2, kinds, levels, 1, width), full),
             pltpu.VMEM((STEPS, 2, kinds, levels, rows, 128), full),
-            *pairs,
+            *semaphores,
             dma((6 + levels,)),
         ],
         compiler_params=pltpu.CompilerParams(

time: 88.7 us -> 79.7 us (0.90)
  Pallas kernels: 87.5 us -> 78.3 us
    pallas_call x1, Pallas kernels: 87.5 us -> 78.3 us  [on_device(): pl.pallas_call(kernel, out_shape=jax.ShapeDtypeStruct((kinds, levels, row...]
where the time goes in v3:
time: 79.7 us; the launch traced here: 79.3 us
  Pallas kernels  78.3 us (98%)
  local copies, waits for them, and re-layouts  1.02 us (1%)
    pallas_call x1, Pallas kernels, on_device(): pl.pallas_call(kernel, out_shape=jax.ShapeDtypeStruct((kinds, levels, row...  78.3 us

profile of v3, /device:TPU:0, one launch (start us, length us, event | category | flops | bytes accessed | tf_op | source)
XLA Modules:
  0.0 79.3 jit_solution(14095192182629203322)
XLA Ops:
  0.0 78.3 %increment.1 = f32[3,3,32,1024]{3,2,1,0:T(8,128)S(1)} custom-call(bf16[2,3,32,2048]{3,2,1,0:T(8,128)(2,1)} %control.1, bf16[3,2,3,32,2048]{4,3,2,1,0:T(8,128)(2,1)} %pert.1, bf16[256,2048]{1,0:T(8,128)(2,1)} %taper.1, bf16[32,256]{1,0:T(8,128)(2,1)} %row_part.1, f32[3,3,32,1024]{3,2,1,0:T(8,128)} %courant_in.1, f32[2,3,32,1024]{3,2,1,0:T(8,128)} %slope_in.1), custom_call_target="tpu_custom_call" | custom-call | tf_op jit(solution)/shard_map/increment/pallas_call | solution.py:554
  78.3 1.0 %copy.8 = f32[3,3,32,1024]{3,2,1,0:T(8,128)} copy(f32[3,3,32,1024]{3,2,1,0:T(8,128)S(1)} %increment.1) | data formatting | bytes 2359296

commit v4 on v3

--- a/solution.py
+++ b/solution.py
@@ -102,9 +102,28 @@
         part = taper_all.at[pl.ds(0, count - 1), pl.ds(0, share), pl.ds(0, lanes)]
         return remote(part, part, side_send.at[0], side_recv.at[0], row=peer_of(1))
 
-    def all_lev():
-        part = taper_all.at[pl.ds(0, count - 1), pl.ds(0, share)]
+    def all_lev(blocks):
+        part = taper_all.at[pl.ds(0, blocks), pl.ds(0, share)]
         return remote(part, part, lev_send.at[0], lev_recv.at[0], lev=levs - 1 - lev_at)
+
+    corners = inner > 1 and levs > 1 and outer > 1
+    at_end = (line_at == 0) | (line_at == outer - 1)
+    far = jnp.where(line_at == 0, outer - 1, 0) * inner + inner - 1
+
+    def corner(lev):
+        part = piece(far, lev, side_at)
+        return remote(part, part, lev_send.at[1], lev_recv.at[1], lev=levs - 1 - lev_at)
+
+    def opposite(at):
+        part = piece(far, levs - 1 - lev_at, at)
+        return remote(part, part, first_send.at[1], first_recv.at[1], row=other)
+
+    def each_lev(action):
+        if corners:
+            pl.when(at_end)(lambda: action(all_lev(count - 2)))
+            pl.when(jnp.logical_not(at_end))(lambda: action(all_lev(count - 1)))
+        else:
+            action(all_lev(count - 1))
 
     def pert_copy(peer, slot):
         return remote(
@@ -396,7 +415,11 @@
                 send(onwards, relay)
             if inner > 1:
                 start(there, lambda origin=origin: side(origin, side_at))
-            across(there, origin, side_at)
+            if corners and hop == outer - 2:
+                across(there & (side_at == turn), origin, side_at)
+                start(there & (side_at != turn), lambda: corner(lev_at))
+            else:
+                across(there, origin, side_at)
 
     def side_step(hop):
         for turn in range(inner):
@@ -408,7 +431,16 @@
                         side(origin, inner - 1 - side_at).wait_recv()
 
                     when(there, arrived)
-                    across(there, origin, inner - 1 - side_at)
+                    if corners and hop == outer - 2:
+                        across(there & (side_at == turn), origin, inner - 1 - side_at)
+                    else:
+                        across(there, origin, inner - 1 - side_at)
+        if corners and hop == outer - 2:
+
+            @pl.when(at_end)
+            def _():
+                corner(levs - 1 - lev_at).wait_recv()
+                opposite(side_at).start()
 
     span = min(width, 256)
 
@@ -475,7 +507,12 @@
             if inner > 1:
                 all_side().wait_send()
             if levs > 1:
-                all_lev().wait_recv()
+                each_lev(lambda copy: copy.wait_recv())
+            if corners:
+
+                @pl.when(at_end)
+                def _():
+                    opposite(inner - 1 - side_at).wait_recv()
         for shift in range(1, mems):
             peer = (mem_at + shift) % mems
             pert_copy(peer, peer).wait_recv()
@@ -484,37 +521,60 @@
         if count > 1:
             all_sent(two_send.at[0]).wait_send()
             if levs > 1:
-                all_lev().wait_send()
+                each_lev(lambda copy: copy.wait_send())
+            if corners:
+
+                @pl.when(at_end)
+                def _():
+                    corner(lev_at).wait_send()
+                    opposite(side_at).wait_send()
         for level in range(levels):
             for shift in range(1, mems):
                 onward((mem_at + shift) % mems, level, mem_at).wait_send()
 
     first_step()
     chunks = [(turn, half) for turn in range(1, levels) for half in range(2)]
-    turns_left, rows_known = list(range(levels)), False
+    turns_left = list(range(levels))
+
+    def next_chunk():
+        if chunks:
+            one_chunk(*chunks.pop(0))
+
+    def next_row():
+        if turns_left:
+            turn = turns_left.pop(0)
+            while chunks and chunks[0][0] <= turn:
+                next_chunk()
+            if turn == 0:
+                whole_row()
+            row_step(turn)
+
     for hop in range(outer - 1):
-        for turn in range(inner):
+        hop_step(hop, 0)
+        if hop == 0:
+            next_chunk()
+            other_step()
+        if hop == 1:
+            side_step(0)
+        for turn in range(1, inner):
             hop_step(hop, turn)
-            if chunks:
-                one_chunk(*chunks.pop(0))
-            if hop == 0 and turn == 0:
-                other_step()
-        if hop > 0 and not chunks and turns_left:
-            if not rows_known:
-                whole_row()
-                rows_known = True
-            row_step(turns_left.pop(0))
-        side_step(hop)
-        if 0 < hop < outer - 2 and rows_known and turns_left:
-            row_step(turns_left.pop(0))
+        if hop == 0:
+            next_chunk()
+            if outer == 2:
+                side_step(0)
+        elif hop < outer - 2:
+            next_chunk()
+            side_step(hop)
+            next_row()
+            next_chunk()
+            next_row()
+        else:
+            next_row()
+            side_step(hop)
     if outer == 1:
         other_step()
-    for turn, half in chunks:
-        one_chunk(turn, half)
-    if not rows_known:
-        whole_row()
-    for turn in turns_left:
-        row_step(turn)
+    for _ in range(levels):
+        next_row()
     for turn in range(levels - 1):
         back_step(turn)
     taper_whole()
@@ -547,8 +607,8 @@
     inner = 2 if count % 2 == 0 else 1
     sides, hops = max(1, min(2, mems - 1)), max(1, count // inner - 1)
     semaphores = [dma((1,)), dma((levels,)), dma((1,)), dma((1,)), dma((1,)), dma((levels,))]
-    semaphores += [dma((mems, levels))] * 2 + [dma((mems,))] * 2 + [dma((1,))] * 2
-    semaphores += [dma((2, hops, inner))] * 2 + [dma((1,)), dma((count,)), dma((1,)), dma((1,))]
+    semaphores += [dma((mems, levels))] * 2 + [dma((mems,))] * 2 + [dma((2,))] * 2
+    semaphores += [dma((2, hops, inner))] * 2 + [dma((1,)), dma((count,)), dma((2,)), dma((2,))]
     semaphores += [dma((STEPS,)), dma((2, kinds)), dma((STEPS, 2)), dma((2, 2, kinds + 1))]
     semaphores += [dma((STEPS, sides)), dma((2, sides, kinds + 1))]
     return pl.pallas_call(

time: 79.7 us -> 76.5 us (0.960)
  Pallas kernels: 78.3 us -> 75.3 us
    pallas_call x1, Pallas kernels: 78.3 us -> 75.3 us  [on_device(): pl.pallas_call(kernel, out_shape=jax.ShapeDtypeStruct((kinds, levels, row...]
where the time goes in v4:
time: 76.5 us; the launch traced here: 76.4 us
  Pallas kernels  75.3 us (98%)
  local copies, waits for them, and re-layouts  1.02 us (1%)
    pallas_call x1, Pallas kernels, on_device(): pl.pallas_call(kernel, out_shape=jax.ShapeDtypeStruct((kinds, levels, row...  75.3 us

profile of v4, /device:TPU:0, one launch (start us, length us, event | category | flops | bytes accessed | tf_op | source)
XLA Modules:
  0.0 76.4 jit_solution(14169021610507417131)
XLA Ops:
  0.0 75.3 %increment.1 = f32[3,3,32,1024]{3,2,1,0:T(8,128)S(1)} custom-call(bf16[2,3,32,2048]{3,2,1,0:T(8,128)(2,1)} %control.1, bf16[3,2,3,32,2048]{4,3,2,1,0:T(8,128)(2,1)} %pert.1, bf16[256,2048]{1,0:T(8,128)(2,1)} %taper.1, bf16[32,256]{1,0:T(8,128)(2,1)} %row_part.1, f32[3,3,32,1024]{3,2,1,0:T(8,128)} %courant_in.1, f32[2,3,32,1024]{3,2,1,0:T(8,128)} %slope_in.1), custom_call_target="tpu_custom_call" | custom-call | tf_op jit(solution)/shard_map/increment/pallas_call | solution.py:614
  75.3 1.0 %copy.8 = f32[3,3,32,1024]{3,2,1,0:T(8,128)} copy(f32[3,3,32,1024]{3,2,1,0:T(8,128)S(1)} %increment.1) | data formatting | bytes 2359296

commit v5 on v4

--- a/solution.py
+++ b/solution.py
@@ -565,8 +565,8 @@
         elif hop < outer - 2:
             next_chunk()
             side_step(hop)
+            next_chunk()
             next_row()
-            next_chunk()
             next_row()
         else:
             next_row()

time: 76.5 us -> 75.6 us (0.988)
  Pallas kernels: 75.3 us -> 74.4 us
    pallas_call x1, Pallas kernels: 75.3 us -> 74.4 us  [on_device(): pl.pallas_call(kernel, out_shape=jax.ShapeDtypeStruct((kinds, levels, row...]
where the time goes in v5:
time: 75.6 us; the launch traced here: 75.4 us
  Pallas kernels  74.4 us (98%)
  local copies, waits for them, and re-layouts  1.02 us (1%)
    pallas_call x1, Pallas kernels, on_device(): pl.pallas_call(kernel, out_shape=jax.ShapeDtypeStruct((kinds, levels, row...  74.4 us

profile of v5, /device:TPU:0, one launch (start us, length us, event | category | flops | bytes accessed | tf_op | source)
XLA Modules:
  0.0 75.4 jit_solution(11481028811350116143)
XLA Ops:
  0.0 74.4 %increment.1 = f32[3,3,32,1024]{3,2,1,0:T(8,128)S(1)} custom-call(bf16[2,3,32,2048]{3,2,1,0:T(8,128)(2,1)} %control.1, bf16[3,2,3,32,2048]{4,3,2,1,0:T(8,128)(2,1)} %pert.1, bf16[256,2048]{1,0:T(8,128)(2,1)} %taper.1, bf16[32,256]{1,0:T(8,128)(2,1)} %row_part.1, f32[3,3,32,1024]{3,2,1,0:T(8,128)} %courant_in.1, f32[2,3,32,1024]{3,2,1,0:T(8,128)} %slope_in.1), custom_call_target="tpu_custom_call" | custom-call | tf_op jit(solution)/shard_map/increment/pallas_call | solution.py:614
  74.4 1.0 %copy.8 = f32[3,3,32,1024]{3,2,1,0:T(8,128)} copy(f32[3,3,32,1024]{3,2,1,0:T(8,128)S(1)} %increment.1) | data formatting | bytes 2359296
